TPU v7x, 256 devices: a whole 4x4x8 slice. The times are simulated.
256 devices in a mesh: kpt: 16 (over y, x), pw: 16 (over z, core).
Axes of the slice: x: 4, y: 4, z: 8, core: 2. Of those that a mesh axis runs over, the one named last changes fastest.
Arguments:
- energies: float32 [64, 512], P('kpt', 'pw'), may hold values from 0.5 to 3
- current: float32 [2, 64, 512], P(None, 'kpt', 'pw'), may hold values from -40 to 40
- previous: float32 [2, 64, 512], P(None, 'kpt', 'pw'), may hold values from -6 to 6
- previous_beta: float32 [2], replicated, may hold values from 0.5 to 2
- pair_left: bfloat16 [64, 512, 4096], P('kpt', None, 'pw'), may hold values from -0.09375 to 0.09375
- pair_right: bfloat16 [64, 512, 4096], P('kpt', None, 'pw'), may hold values from -0.25 to 0.25
- screened: bfloat16 [64, 4096, 4096], P('kpt', 'pw'), may hold values from -0.01171875 to 0.01171875
- momentum_index: int32 [64, 64], replicated, may hold values from 0 to 63, each once within a row
Outputs:
- last_vector: float32 [2, 64, 512], P(None, 'kpt', 'pw')
- prior_vector: float32 [2, 64, 512], P(None, 'kpt', 'pw')
- alpha_terms: float32 [2, 3], replicated
- beta_terms: float32 [2, 3], replicated
Inputs may be any that keep to these rules, and one draw needn't show every extreme that they name: Each row of momentum_index names every index from 0 to 63 once.
All inputs are finite; a program needn't handle non-finite values.
Results may differ from a plain program's by a relative error of at most 0.003.
Values may be sent and summed in bfloat16 or wider, within the bound.
A program may use at most 128 MiB of HBM per device.

v0:
```python
import functools

import jax
import jax.numpy as jnp
from jax import lax
from jax.sharding import Mesh
from jax.sharding import PartitionSpec as P

STEPS = 3
KPT = ("kpt_0", "kpt_1")
PW = ("pw_0", "pw_1")
KPT_PW = ("kpt_0", "kpt_1", "pw_0", "pw_1")


epsilon = 1e-06


def laid_out(blocks, dim):
    lengths = list(blocks.shape[1:])
    lengths[dim] *= blocks.shape[0]
    return jnp.moveaxis(blocks, 0, dim).reshape(lengths)


def sent_to_all(x, axis):
    copies = jnp.broadcast_to(x, (lax.axis_size(axis), *x.shape))
    return lax.all_to_all(copies, axis, split_axis=0, concat_axis=0, tiled=True)


def collect(x, axis, dim):
    return laid_out(sent_to_all(x, axis), dim)


def rows_first(arrays, axis, dims):
    turned = [jnp.moveaxis(a, dim, 0) for a, dim in zip(arrays, dims)]
    both = jnp.concatenate([t.reshape(len(t), -1) for t in turned], axis=1)
    out, at, done = (lax.all_gather(both, axis, axis=0, tiled=True), 0, [])
    for t, dim in zip(turned, dims):
        share = out[:, at : at + t[0].size].reshape(-1, *t.shape[1:])
        done.append(jnp.moveaxis(share, 0, dim))
        at += t[0].size
    return tuple(done)


def cut_along(x, dim, count):
    before, after = (x.shape[:dim], x.shape[dim + 1 :])
    return jnp.moveaxis(x.reshape(*before, count, -1, *after), dim, 0)


def summed_on_arrival(x, axis, dim):
    blocks = cut_along(x, dim, lax.axis_size(axis))
    arrived = lax.all_to_all(blocks, axis, split_axis=0, concat_axis=0, tiled=True)
    return arrived.sum(axis=0)


def taken_together(x, axis):
    return sent_to_all(x, axis).sum(axis=0)


def over_axes(x, axes):
    return functools.reduce(lax.psum, axes, x)


def own_bands(array, offset, width):
    return lax.dynamic_slice_in_dim(array, offset, width, 2)


def screened_images(density, screened):
    kpoint_rows = collect(density, KPT, 0)
    return jnp.einsum(
        "qsg,kvg->qkvs", screened, collect(kpoint_rows, PW, 2), preferred_element_type=jnp.float32
    )


def on_device(
    energies, current, previous, previous_beta, pair_left, pair_right, screened, momentum_index
):
    kpoint_total = momentum_index.shape[0]
    band_total = pair_left.shape[1]
    entries = kpoint_total * band_total
    band_width = band_total // lax.axis_size(PW)
    band_offset = lax.axis_index(PW) * band_width
    qcount = screened.shape[0]
    qpoints = lax.axis_index(KPT) * qcount + jnp.arange(qcount, dtype=jnp.int32)
    selector = (momentum_index[None, :, :] == qpoints[:, None, None]).astype(jnp.float32)
    vector, earlier, levels = rows_first((current, previous, energies), PW, (2, 2, 1))
    beta_before = previous_beta
    alpha_list = []
    beta_list = []
    for turn_index in range(STEPS):
        rounded = vector.astype(jnp.bfloat16)
        density = jnp.einsum(
            "kcg,vkc->kvg", pair_right, rounded, preferred_element_type=jnp.float32
        ).astype(jnp.bfloat16)
        images = screened_images(density, screened)
        partial_field = jnp.einsum(
            "qjk,qkvs->jvs",
            selector,
            images,
            precision=lax.Precision.HIGHEST,
            preferred_element_type=jnp.float32,
        )
        potential = summed_on_arrival(partial_field, KPT, 0).astype(jnp.bfloat16)
        partial_direct = jnp.einsum(
            "kcs,kvs->vkc", pair_left, potential, preferred_element_type=jnp.float32
        )
        direct = taken_together(partial_direct, PW)
        applied = levels[None] * vector - direct - beta_before[:, None, None] * earlier
        vector_own = own_bands(vector, band_offset, band_width)
        applied_own = own_bands(applied, band_offset, band_width)
        cross_sum, square_sum, vector_sum = (
            over_axes(jnp.sum(vector_own * applied_own, axis=(1, 2)), KPT_PW),
            over_axes(jnp.sum(applied_own * applied_own, axis=(1, 2)), KPT_PW),
            over_axes(jnp.sum(vector_own * vector_own, axis=(1, 2)), KPT_PW),
        )
        alpha_now = cross_sum / entries
        mean_square = (
            square_sum / entries
            - 2.0 * alpha_now * (cross_sum / entries)
            + alpha_now * alpha_now * (vector_sum / entries)
        )
        beta_now = jnp.sqrt(mean_square + epsilon)
        residual = applied - alpha_now[:, None, None] * vector
        earlier = vector
        vector = residual / beta_now[:, None, None]
        beta_before = beta_now
        alpha_list.append(alpha_now)
        beta_list.append(beta_now)
    last_vector = own_bands(vector, band_offset, band_width)
    prior_vector = own_bands(earlier, band_offset, band_width)
    return (last_vector, prior_vector, jnp.stack(alpha_list, axis=1), jnp.stack(beta_list, axis=1))


def solution(mesh):
    finer = Mesh(mesh.devices.reshape(4, 4, 8, 2), ("kpt_0", "kpt_1", "pw_0", "pw_1"))
    in_specs = (
        P(KPT, PW),
        P(None, KPT, PW),
        P(None, KPT, PW),
        P(),
        P(KPT, None, PW),
        P(KPT, None, PW),
        P(KPT, PW, None),
        P(),
    )
    out_specs = (P(None, KPT, PW), P(None, KPT, PW), P(), P())
    return jax.shard_map(
        on_device, mesh=finer, in_specs=in_specs, out_specs=out_specs, check_vma=False
    )
```

profile of v0, /device:TPU:1, one launch (start us, length us, event | category | flops | bytes accessed | tf_op | source)
XLA Modules:
  0.0 373.9 jit_solution(12473416637905957974)
XLA Ops:
  0.6 0.8 maximum_bitcast_fusion
  1.5 21.8 %all-gather = f32[16,32,20]{1,2,0:T(8,128)S(1)} all-gather(f32[1,32,20]{1,2,0:T(8,128)S(1)} %maximum_bitcast_fusion), channel_id=1, replica_groups=mesh['kpt_0'=4,'kpt_1'=4,'pw_0'=8,'pw_1'=2] {'pw_0','pw_1'}, dimensions={0}, use_global_device_ids=true | all-gather | bytes 43520 | tf_op jit(solution)/shard_map/all_gather | solution.py:36
  23.3 0.1 reshape.74
  23.5 1.5 convolution_convert_fusion.2
  25.0 13.1 %all_to_all.60 = bf16[16,4,2,256]{3,1,2,0:T(4,128)(2,1)S(1)} all-to-all(bf16[16,4,2,256]{3,1,2,0:T(4,128)(2,1)S(1)} %broadcast_in_dim.18), channel_id=1, replica_groups=mesh['kpt_0'=4,'kpt_1'=4,'pw_0'=8,'pw_1'=2] {'kpt_0','kpt_1'}, dimensions={0} | all-to-all | bytes 131072 | tf_op jit(solution)/shard_map/all_to_all | solution.py:26
  38.1 1.1 broadcast_in_dim.19
  39.2 5.4 %all-to-all-start.1 = ((bf16[16,64,2,256]{3,1,2,0:T(8,128)(2,1)}), bf16[16,64,2,256]{3,1,2,0:T(8,128)(2,1)S(1)}, u32[]{:S(2)}, u32[]{:S(2)}) async-start(bf16[16,64,2,256]{3,1,2,0:T(8,128)(2,1)} %broadcast_in_dim.19), calls=%async_computation.1 | async-start | bytes 2097152 | tf_op jit(solution)/shard_map/all_to_all | solution.py:26
  44.6 28.0 %all-to-all-done.1 = bf16[16,64,2,256]{3,1,2,0:T(8,128)(2,1)S(1)} async-done(((bf16[16,64,2,256]{3,1,2,0:T(8,128)(2,1)}), bf16[16,64,2,256]{3,1,2,0:T(8,128)(2,1)S(1)}, u32[]{:S(2)}, u32[]{:S(2)}) %all-to-all-start.1) | async-done | bytes 1048608 | tf_op jit(solution)/shard_map/all_to_all | solution.py:26
  72.6 1.6 copy.169
  74.2 1.6 reshape.75
  75.8 6.3 %fusion.6 = f32[4,64,2,256]{3,1,0,2:T(8,128)S(1)} fusion(bf16[4,256,4096]{2,1,0:T(8,128)(2,1)} %param.14, bf16[64,2,4096,1]{2,0,1,3:T(8,128)(2,1)S(1)} %reshape.75), kind=kOutput, calls=%fused_computation.6 | convolution fusion | flops 1073741824 | bytes 9961472 | tf_op jit(solution)/shard_map/qsg,kvg->qkvs/dot_general | solution.py:69
  82.1 0.4 convolution_bitcast_fusion.2
  82.5 9.7 %all_to_all.61 = f32[16,4,2,256]{3,1,2,0:T(4,128)S(1)} all-to-all(f32[16,4,2,256]{3,1,2,0:T(4,128)S(1)} %copy.170), channel_id=1, replica_groups=mesh['kpt_0'=4,'kpt_1'=4,'pw_0'=8,'pw_1'=2] {'kpt_0','kpt_1'}, dimensions={0} | all-to-all | bytes 262144 | tf_op jit(solution)/shard_map/all_to_all | solution.py:51
  92.3 0.4 convolution_bitcast_fusion.5
  92.7 0.8 broadcast_in_dim.20
  93.5 4.8 %all-to-all-start.3 = ((f32[16,2,4,512]{3,2,1,0:T(4,128)}), f32[16,2,4,512]{3,2,1,0:T(4,128)S(1)}, u32[]{:S(2)}, u32[]{:S(2)}) async-start(f32[16,2,4,512]{3,2,1,0:T(4,128)} %broadcast_in_dim.20), calls=%async_computation.3 | async-start | bytes 524288 | tf_op jit(solution)/shard_map/all_to_all | solution.py:26
  98.3 11.6 %all-to-all-done.3 = f32[16,2,4,512]{3,2,1,0:T(4,128)S(1)} async-done(((f32[16,2,4,512]{3,2,1,0:T(4,128)}), f32[16,2,4,512]{3,2,1,0:T(4,128)S(1)}, u32[]{:S(2)}, u32[]{:S(2)}) %all-to-all-start.3) | async-done | bytes 262176 | tf_op jit(solution)/shard_map/all_to_all | solution.py:26
  109.9 0.1 bitcast_subtract_fusion
  110.0 0.2 multiply_reduce_fusion.6
  110.2 6.6 %all-reduce.8 = (f32[2]{0:T(128)S(1)}, f32[2]{0:T(128)S(1)}, f32[2]{0:T(128)S(1)}) all-reduce(f32[2]{0:T(128)S(1)} %get-tuple-element.39, f32[2]{0:T(128)S(1)} %get-tuple-element.38, f32[2]{0:T(128)S(1)} %get-tuple-element.37), channel_id=1, replica_groups=mesh['kpt_0'=4,'kpt_1'=4,'pw_0'=8,'pw_1'=2] {'kpt_0'}, use_global_device_ids=true, to_apply=%region_13.0 | all-reduce | flops 6 | bytes 48 | tf_op jit(solution)/shard_map/psum | solution.py:60
  116.8 6.9 %all-reduce.5 = (f32[2]{0:T(128)S(1)}, f32[2]{0:T(128)S(1)}, f32[2]{0:T(128)S(1)}) all-reduce(f32[2]{0:T(128)S(1)} %get-tuple-element.65, f32[2]{0:T(128)S(1)} %get-tuple-element.66, f32[2]{0:T(128)S(1)} %get-tuple-element.67), channel_id=1, replica_groups=mesh['kpt_0'=4,'kpt_1'=4,'pw_0'=8,'pw_1'=2] {'kpt_1'}, use_global_device_ids=true, to_apply=%region_14.0 | all-reduce | flops 6 | bytes 48 | tf_op jit(solution)/shard_map/psum | solution.py:60
  123.7 10.7 %all-reduce.2 = (f32[2]{0:T(128)S(1)}, f32[2]{0:T(128)S(1)}, f32[2]{0:T(128)S(1)}) all-reduce(f32[2]{0:T(128)S(1)} %get-tuple-element.56, f32[2]{0:T(128)S(1)} %get-tuple-element.57, f32[2]{0:T(128)S(1)} %get-tuple-element.58), channel_id=1, replica_groups=mesh['kpt_0'=4,'kpt_1'=4,'pw_0'=8,'pw_1'=2] {'pw_0'}, use_global_device_ids=true, to_apply=%region_15.0 | all-reduce | flops 6 | bytes 48 | tf_op jit(solution)/shard_map/psum | solution.py:60
  134.4 9.7 %all-reduce.11 = (f32[2]{0:T(128)S(1)}, f32[2]{0:T(128)S(1)}, f32[2]{0:T(128)S(1)}) all-reduce(f32[2]{0:T(128)S(1)} %get-tuple-element.47, f32[2]{0:T(128)S(1)} %get-tuple-element.48, f32[2]{0:T(128)S(1)} %get-tuple-element.49), channel_id=1, replica_groups=mesh['kpt_0'=4,'kpt_1'=4,'pw_0'=8,'pw_1'=2] {'pw_1'}, use_global_device_ids=true, to_apply=%region_16.0 | all-reduce | flops 6 | bytes 48 | tf_op jit(solution)/shard_map/psum | solution.py:60
  144.0 0.1 fusion.46
  144.1 0.2 convolution_convert_fusion.1
  144.4 9.1 %all_to_all.62 = bf16[16,4,2,256]{3,1,2,0:T(4,128)(2,1)S(1)} all-to-all(bf16[16,4,2,256]{3,1,2,0:T(4,128)(2,1)S(1)} %broadcast_in_dim.21), channel_id=1, replica_groups=mesh['kpt_0'=4,'kpt_1'=4,'pw_0'=8,'pw_1'=2] {'kpt_0','kpt_1'}, dimensions={0} | all-to-all | bytes 131072 | tf_op jit(solution)/shard_map/all_to_all | solution.py:26
  153.6 0.1 broadcast_in_dim.22
  153.7 35.2 %all_to_all.63 = bf16[16,64,2,256]{3,1,2,0:T(8,128)(2,1)S(1)} all-to-all(bf16[16,64,2,256]{3,1,2,0:T(8,128)(2,1)S(1)} %broadcast_in_dim.22), channel_id=1, replica_groups=mesh['kpt_0'=4,'kpt_1'=4,'pw_0'=8,'pw_1'=2] {'pw_0','pw_1'}, dimensions={0} | all-to-all | bytes 2097152 | tf_op jit(solution)/shard_map/all_to_all | solution.py:26
  188.9 1.6 copy.179
  190.5 1.6 reshape.79
  192.1 6.3 %fusion.9 = f32[4,64,2,256]{3,1,0,2:T(8,128)S(1)} fusion(bf16[4,256,4096]{2,1,0:T(8,128)(2,1)} %param.14, bf16[64,2,4096,1]{2,0,1,3:T(8,128)(2,1)S(1)} %reshape.79), kind=kOutput, calls=%fused_computation.7 | convolution fusion | flops 1073741824 | bytes 9961472 | tf_op jit(solution)/shard_map/qsg,kvg->qkvs/dot_general | solution.py:69
  198.3 0.4 convolution_bitcast_fusion.1
  198.8 10.0 %all_to_all.64 = f32[16,4,2,256]{3,1,2,0:T(4,128)S(1)} all-to-all(f32[16,4,2,256]{3,1,2,0:T(4,128)S(1)} %copy.180), channel_id=1, replica_groups=mesh['kpt_0'=4,'kpt_1'=4,'pw_0'=8,'pw_1'=2] {'kpt_0','kpt_1'}, dimensions={0} | all-to-all | bytes 262144 | tf_op jit(solution)/shard_map/all_to_all | solution.py:51
  208.8 0.4 convolution_bitcast_fusion.4
  209.2 0.1 broadcast_in_dim.46
  209.3 15.5 %all_to_all.65 = f32[16,2,4,512]{3,2,1,0:T(4,128)S(1)} all-to-all(f32[16,2,4,512]{3,2,1,0:T(4,128)S(1)} %broadcast_in_dim.46), channel_id=1, replica_groups=mesh['kpt_0'=4,'kpt_1'=4,'pw_0'=8,'pw_1'=2] {'pw_0','pw_1'}, dimensions={0} | all-to-all | bytes 524288 | tf_op jit(solution)/shard_map/all_to_all | solution.py:26
  224.8 0.1 fusion.33
  224.9 0.2 multiply_reduce_fusion.4
  225.1 6.6 %all-reduce.7 = (f32[2]{0:T(128)S(1)}, f32[2]{0:T(128)S(1)}, f32[2]{0:T(128)S(1)}) all-reduce(f32[2]{0:T(128)S(1)} %get-tuple-element.36, f32[2]{0:T(128)S(1)} %get-tuple-element.35, f32[2]{0:T(128)S(1)} %get-tuple-element.34), channel_id=1, replica_groups=mesh['kpt_0'=4,'kpt_1'=4,'pw_0'=8,'pw_1'=2] {'kpt_0'}, use_global_device_ids=true, to_apply=%region_30.0 | all-reduce | flops 6 | bytes 48 | tf_op jit(solution)/shard_map/psum | solution.py:60
  231.7 6.9 %all-reduce.4 = (f32[2]{0:T(128)S(1)}, f32[2]{0:T(128)S(1)}, f32[2]{0:T(128)S(1)}) all-reduce(f32[2]{0:T(128)S(1)} %get-tuple-element.62, f32[2]{0:T(128)S(1)} %get-tuple-element.63, f32[2]{0:T(128)S(1)} %get-tuple-element.64), channel_id=1, replica_groups=mesh['kpt_0'=4,'kpt_1'=4,'pw_0'=8,'pw_1'=2] {'kpt_1'}, use_global_device_ids=true, to_apply=%region_31.0 | all-reduce | flops 6 | bytes 48 | tf_op jit(solution)/shard_map/psum | solution.py:60
  238.6 10.7 %all-reduce.1 = (f32[2]{0:T(128)S(1)}, f32[2]{0:T(128)S(1)}, f32[2]{0:T(128)S(1)}) all-reduce(f32[2]{0:T(128)S(1)} %get-tuple-element.53, f32[2]{0:T(128)S(1)} %get-tuple-element.54, f32[2]{0:T(128)S(1)} %get-tuple-element.55), channel_id=1, replica_groups=mesh['kpt_0'=4,'kpt_1'=4,'pw_0'=8,'pw_1'=2] {'pw_0'}, use_global_device_ids=true, to_apply=%region_32.0 | all-reduce | flops 6 | bytes 48 | tf_op jit(solution)/shard_map/psum | solution.py:60
  249.3 9.7 %all-reduce.10 = (f32[2]{0:T(128)S(1)}, f32[2]{0:T(128)S(1)}, f32[2]{0:T(128)S(1)}) all-reduce(f32[2]{0:T(128)S(1)} %get-tuple-element.44, f32[2]{0:T(128)S(1)} %get-tuple-element.45, f32[2]{0:T(128)S(1)} %get-tuple-element.46), channel_id=1, replica_groups=mesh['kpt_0'=4,'kpt_1'=4,'pw_0'=8,'pw_1'=2] {'pw_1'}, use_global_device_ids=true, to_apply=%region_33.0 | all-reduce | flops 6 | bytes 48 | tf_op jit(solution)/shard_map/psum | solution.py:60
  259.0 0.1 fusion.45
  259.0 0.2 convolution_convert_fusion
  259.3 9.1 %all_to_all.66 = bf16[16,4,2,256]{3,1,2,0:T(4,128)(2,1)S(1)} all-to-all(bf16[16,4,2,256]{3,1,2,0:T(4,128)(2,1)S(1)} %broadcast_in_dim.47), channel_id=1, replica_groups=mesh['kpt_0'=4,'kpt_1'=4,'pw_0'=8,'pw_1'=2] {'kpt_0','kpt_1'}, dimensions={0} | all-to-all | bytes 131072 | tf_op jit(solution)/shard_map/all_to_all | solution.py:26
  268.5 0.1 broadcast_in_dim.48
  268.6 35.2 %all_to_all.67 = bf16[16,64,2,256]{3,1,2,0:T(8,128)(2,1)S(1)} all-to-all(bf16[16,64,2,256]{3,1,2,0:T(8,128)(2,1)S(1)} %broadcast_in_dim.48), channel_id=1, replica_groups=mesh['kpt_0'=4,'kpt_1'=4,'pw_0'=8,'pw_1'=2] {'pw_0','pw_1'}, dimensions={0} | all-to-all | bytes 2097152 | tf_op jit(solution)/shard_map/all_to_all | solution.py:26
  303.8 0.6 copy.189
  304.4 0.5 reshape.81
  305.0 6.3 %fusion.12 = f32[4,64,2,256]{3,1,0,2:T(8,128)S(1)} fusion(bf16[4,256,4096]{2,1,0:T(8,128)(2,1)} %param.14, bf16[64,2,4096,1]{2,0,1,3:T(8,128)(2,1)S(1)} %reshape.81), kind=kOutput, calls=%fused_computation.8 | convolution fusion | flops 1073741824 | bytes 9961472 | tf_op jit(solution)/shard_map/qsg,kvg->qkvs/dot_general | solution.py:69
  311.2 0.4 convolution_bitcast_fusion
  311.7 10.0 %all_to_all.68 = f32[16,4,2,256]{3,1,2,0:T(4,128)S(1)} all-to-all(f32[16,4,2,256]{3,1,2,0:T(4,128)S(1)} %copy.190), channel_id=1, replica_groups=mesh['kpt_0'=4,'kpt_1'=4,'pw_0'=8,'pw_1'=2] {'kpt_0','kpt_1'}, dimensions={0} | all-to-all | bytes 262144 | tf_op jit(solution)/shard_map/all_to_all | solution.py:51
  321.7 0.4 convolution_bitcast_fusion.3
  322.1 0.1 broadcast_in_dim.49
  322.2 15.5 %all_to_all.69 = f32[16,2,4,512]{3,2,1,0:T(4,128)S(1)} all-to-all(f32[16,2,4,512]{3,2,1,0:T(4,128)S(1)} %broadcast_in_dim.49), channel_id=1, replica_groups=mesh['kpt_0'=4,'kpt_1'=4,'pw_0'=8,'pw_1'=2] {'pw_0','pw_1'}, dimensions={0} | all-to-all | bytes 524288 | tf_op jit(solution)/shard_map/all_to_all | solution.py:26
  337.7 0.1 multiply_subtract_fusion
  337.8 0.2 multiply_reduce_fusion.1
  338.0 6.6 %all-reduce.6 = (f32[2]{0:T(128)S(1)}, f32[2]{0:T(128)S(1)}, f32[2]{0:T(128)S(1)}) all-reduce(f32[2]{0:T(128)S(1)} %get-tuple-element.40, f32[2]{0:T(128)S(1)} %get-tuple-element.33, f32[2]{0:T(128)S(1)} %get-tuple-element.32), channel_id=1, replica_groups=mesh['kpt_0'=4,'kpt_1'=4,'pw_0'=8,'pw_1'=2] {'kpt_0'}, use_global_device_ids=true, to_apply=%region_47.0 | all-reduce | flops 6 | bytes 48 | tf_op jit(solution)/shard_map/psum | solution.py:60
  344.6 6.9 %all-reduce.3 = (f32[2]{0:T(128)S(1)}, f32[2]{0:T(128)S(1)}, f32[2]{0:T(128)S(1)}) all-reduce(f32[2]{0:T(128)S(1)} %get-tuple-element.59, f32[2]{0:T(128)S(1)} %get-tuple-element.60, f32[2]{0:T(128)S(1)} %get-tuple-element.61), channel_id=1, replica_groups=mesh['kpt_0'=4,'kpt_1'=4,'pw_0'=8,'pw_1'=2] {'kpt_1'}, use_global_device_ids=true, to_apply=%region_48.0 | all-reduce | flops 6 | bytes 48 | tf_op jit(solution)/shard_map/psum | solution.py:60
  351.5 10.7 %all-reduce = (f32[2]{0:T(128)S(1)}, f32[2]{0:T(128)S(1)}, f32[2]{0:T(128)S(1)}) all-reduce(f32[2]{0:T(128)S(1)} %get-tuple-element.50, f32[2]{0:T(128)S(1)} %get-tuple-element.51, f32[2]{0:T(128)S(1)} %get-tuple-element.52), channel_id=1, replica_groups=mesh['kpt_0'=4,'kpt_1'=4,'pw_0'=8,'pw_1'=2] {'pw_0'}, use_global_device_ids=true, to_apply=%region_49.0 | all-reduce | flops 6 | bytes 48 | tf_op jit(solution)/shard_map/psum | solution.py:60
  362.2 9.7 %all-reduce.9 = (f32[2]{0:T(128)S(1)}, f32[2]{0:T(128)S(1)}, f32[2]{0:T(128)S(1)}) all-reduce(f32[2]{0:T(128)S(1)} %get-tuple-element.41, f32[2]{0:T(128)S(1)} %get-tuple-element.42, f32[2]{0:T(128)S(1)} %get-tuple-element.43), channel_id=1, replica_groups=mesh['kpt_0'=4,'kpt_1'=4,'pw_0'=8,'pw_1'=2] {'pw_1'}, use_global_device_ids=true, to_apply=%region_50.0 | all-reduce | flops 6 | bytes 48 | tf_op jit(solution)/shard_map/psum | solution.py:60
  371.9 0.6 copy.195
  372.5 0.6 copy.196
  373.2 0.7 subtract_divide_fusion.1
  (49 shorter events, 0.9 us)
Async XLA Ops:
  0.6 91.7 %copy-start = (bf16[4,512,256]{2,1,0:T(8,128)(2,1)S(1)}, bf16[4,512,256]{2,1,0:T(8,128)(2,1)}, u32[]{:S(2)}) copy-start(bf16[4,512,256]{2,1,0:T(8,128)(2,1)} %param.12) | copy-start | bytes 3145732
  39.2 42.9 %copy-start.2 = (s32[64,64]{1,0:T(8,128)S(1)}, s32[64,64]{1,0:T(8,128)}, u32[]{:S(2)}) copy-start(s32[64,64]{1,0:T(8,128)} %param.15) | copy-start | bytes 49156
  39.2 33.4 %all-to-all-start.1 = ((bf16[16,64,2,256]{3,1,2,0:T(8,128)(2,1)}), bf16[16,64,2,256]{3,1,2,0:T(8,128)(2,1)S(1)}, u32[]{:S(2)}, u32[]{:S(2)}) async-start(bf16[16,64,2,256]{3,1,2,0:T(8,128)(2,1)} %broadcast_in_dim.19), calls=%async_computation.1 | async-start | bytes 2097152 | tf_op jit(solution)/shard_map/all_to_all | solution.py:26
  74.2 35.8 %copy-start.4 = (f32[2]{0:T(128)S(1)}, f32[2]{0:T(128)}, u32[]{:S(2)}) copy-start(f32[2]{0:T(128)} %param.11) | copy-start | bytes 28
  74.2 70.0 %copy-start.1 = (bf16[4,512,256]{2,1,0:T(8,128)(2,1)S(1)}, bf16[4,512,256]{2,1,0:T(8,128)(2,1)}, u32[]{:S(2)}) copy-start(bf16[4,512,256]{2,1,0:T(8,128)(2,1)} %param.13) | copy-start | bytes 3145732
  93.5 16.4 %all-to-all-start.3 = ((f32[16,2,4,512]{3,2,1,0:T(4,128)}), f32[16,2,4,512]{3,2,1,0:T(4,128)S(1)}, u32[]{:S(2)}, u32[]{:S(2)}) async-start(f32[16,2,4,512]{3,2,1,0:T(4,128)} %broadcast_in_dim.20), calls=%async_computation.3 | async-start | bytes 524288 | tf_op jit(solution)/shard_map/all_to_all | solution.py:26
  338.0 35.9 %copy-start.3 = (f32[2,4,32]{2,1,0:T(4,128)}, f32[2,4,32]{2,1,0:T(4,128)S(1)}, u32[]{:S(2)}) copy-start(f32[2,4,32]{2,1,0:T(4,128)S(1)} %get-tuple-element.77) | copy-start | bytes 3076
where the time goes:
time: 375 us; the launch traced here: 374 us
  blocking collectives  286 us (76%)
  waiting for transfers between devices  39.5 us (11%)
  matrix products  23 us (6%)
  local copies, waits for them, and re-layouts  11.6 us (3%)
  starting transfers between devices  10.2 us (3%)
    all_to_all x7, blocking collectives, sent_to_all(): return lax.all_to_all(copies, axis, split_axis=0, concat_axis=0, tiled=True)  133 us
    psum x12, blocking collectives, over_axes(): return functools.reduce(lax.psum, axes, x)  102 us
    all_to_all x2, waiting for transfers between devices, sent_to_all(): return lax.all_to_all(copies, axis, split_axis=0, concat_axis=0, tiled=True)  39.5 us
    all_to_all x3, blocking collectives, summed_on_arrival(): lax.all_to_all(blocks, axis, split_axis=0, concat_axis=0, tiled=True)  29.7 us
    all_gather x1, blocking collectives, rows_first(): out, at, done = (lax.all_gather(both, axis, axis=0, tiled=True), 0, [])  21.8 us
    dot_general x3, matrix products, screened_images(): jnp.einsum('qsg,kvg->qkvs', screened, collect(kpoint_rows, PW, 2), prefer...  18.8 us
    all_to_all x2, starting transfers between devices, sent_to_all(): return lax.all_to_all(copies, axis, split_axis=0, concat_axis=0, tiled=True)  10.2 us
  transfers between devices with their start and end apart: 2, of which 2 were waited for; matrix products, arithmetic and copies ran while one was open for 0% of the time, Pallas kernels for 0%

commit v1 on v0

v1 whole, which is shorter than its diff:
```python
import functools

import jax
import jax.numpy as jnp
from jax import lax
from jax.experimental import pallas as pl
from jax.experimental.pallas import tpu as pltpu
from jax.sharding import Mesh
from jax.sharding import PartitionSpec as P

STEPS = 3
KPT = ("kpt_0", "kpt_1")
PW = ("pw_0", "pw_1")
MESH = pl.DeviceIdType.MESH
F32 = jnp.float32
BF16 = jnp.bfloat16
NT = (((1,), (1,)), ((), ()))

epsilon = 1e-06


def kernel(
    sizes, pack, momentum, left, right, screened,
    last, prior, alphas, betas,
    left_v, right_v, screened_v, selector,
    pk, dens, gath, rows, images, field, field_in, half_out, half_in, direct_z, direct_c, sums,
    vec, old, levels, beta, state,
    load_sem, pk_send, pk_recv, dens_send, dens_recv, gath_send, gath_recv, fwd_send, fwd_recv,
    field_send, field_recv, pair_send, pair_recv, dz_send, dz_recv, dc_send, dc_recv,
    sums_send, sums_recv,
):
    ny, nx, nz = sizes
    na = ny * nx
    nq, width = screened.shape[0], screened.shape[1]
    bands = left.shape[1]
    half = bands // 2
    entries = momentum.shape[0] * bands
    y, x = lax.axis_index("kpt_0"), lax.axis_index("kpt_1")
    z, c = lax.axis_index("pw_0"), lax.axis_index("pw_1")
    other = 1 - c
    a = y * nx + x
    b = z * 2 + c

    def plane_peer(i):
        ty = lax.rem(y + i // nx, ny)
        tx = lax.rem(x + lax.rem(i, nx), nx)
        return ty * nx + tx, (ty, tx, z, c)

    def plane_source(i):
        ty = lax.rem(y + ny - i // nx, ny)
        tx = lax.rem(x + nx - lax.rem(i, nx), nx)
        return ty * nx + tx

    def z_peer(i):
        tz = lax.rem(z + i, nz)
        return tz, (y, x, tz, c)

    def pw_peer(i):
        t = lax.rem(b + i, nz * 2)
        return t, (y, x, t // 2, lax.rem(t, 2))

    partner = (y, x, z, other)

    loads = [
        pltpu.make_async_copy(right, right_v, load_sem.at[0]),
        pltpu.make_async_copy(left, left_v, load_sem.at[1]),
    ]
    for h in range(2):
        for t in range(nz):
            at = (t * 2 + h) * width
            loads.append(
                pltpu.make_async_copy(
                    screened.at[:, :, pl.ds(at, width)],
                    screened_v.at[h, :, :, pl.ds(t * width, width)],
                    load_sem.at[2 + h * nz + t],
                )
            )
    for copy in loads:
        copy.start()

    barrier = pltpu.get_barrier_semaphore()

    @pl.loop(1, na)
    def _(i):
        pl.semaphore_signal(barrier, inc=1, device_id=plane_peer(i)[1], device_id_type=MESH)

    @pl.loop(1, nz * 2)
    def _(i):
        pl.semaphore_signal(barrier, inc=1, device_id=pw_peer(i)[1], device_id_type=MESH)

    nr = na * 8
    nk = momentum.shape[0]
    row = lax.broadcasted_iota(jnp.int32, (nr, nk), 0)
    col = lax.broadcasted_iota(jnp.int32, (nr, nk), 1)
    spread = ((row // 8) * 4 + row % 4 == col).astype(F32).astype(BF16)
    index = momentum[...].astype(F32).astype(BF16)
    by_row = jnp.dot(spread, index, preferred_element_type=F32).astype(BF16)
    by_both = lax.dot_general(by_row, spread, NT, preferred_element_type=F32).astype(jnp.int32)
    r1 = lax.broadcasted_iota(jnp.int32, (nr, nr), 0)
    r2 = lax.broadcasted_iota(jnp.int32, (nr, nr), 1)
    same = (r1 // 4) % 2 == (r2 // 4) % 2
    for q in range(nq):
        hit = jnp.logical_and(by_both == a * nq + q, same)
        selector[:, q * nr : (q + 1) * nr] = jnp.where(hit, 1.0, 0.0).astype(BF16)

    pk[b] = pack[...]
    pl.semaphore_wait(barrier, na - 1 + nz * 2 - 1)

    def pk_copy(i):
        t, device = pw_peer(i)
        return pltpu.make_async_remote_copy(
            pk.at[b], pk.at[b], pk_send.at[t], pk_recv.at[b], device, device_id_type=MESH
        )

    def arrived(ref, sem):
        pltpu.make_async_copy(ref, ref, sem).wait()

    @pl.loop(1, nz * 2)
    def _(i):
        pk_copy(i).start()

    @pl.loop(1, nz * 2)
    def _(i):
        t, _d = pw_peer(i)
        arrived(pk.at[t], pk_recv.at[t])

    lane = lax.broadcasted_iota(jnp.int32, (8, 128), 1)
    for j in range(bands // 128):
        for field_at, ref in ((0, vec), (1, old), (2, levels)):
            total = jnp.zeros((8, 128), F32)
            for m in range(4):
                turned = pk[4 * j + m]
                shift = (32 * (m - field_at)) % 128
                if shift:
                    turned = pltpu.roll(turned, shift, 1)
                total = total + jnp.where(lane // 32 == m, turned, 0.0)
            ref[:, j * 128 : (j + 1) * 128] = total
    beta[...] = jnp.broadcast_to(pack[:, 96:97], (8, 128))

    def own_k(n, k):
        return lax.broadcasted_iota(jnp.int32, (8, n), 0) % 4 == k

    def density_of(t, values):
        high = values.astype(BF16).astype(F32)
        both = jnp.concatenate([high, values - high], axis=0).astype(BF16)
        total = jnp.zeros((8, width), F32)
        for k in range(4):
            out = jnp.dot(both, right_v[k], preferred_element_type=F32)
            total = total + jnp.where(own_k(width, k), out[0:8] + out[8:16], 0.0)
        dens[t, z] = total

        @pl.loop(1, nz)
        def _(i):
            tz, device = z_peer(i)
            pltpu.make_async_remote_copy(
                dens.at[t, z], dens.at[t, z], dens_send.at[t, tz], dens_recv.at[t, z],
                device, device_id_type=MESH,
            ).start()

    def density_arrived(t):
        @pl.loop(1, nz)
        def _(i):
            tz, _d = z_peer(i)
            arrived(dens.at[t, tz], dens_recv.at[t, tz])

    def per_row(tile, at):
        lane_row = tile[:, at : at + 1]
        first = lax.broadcasted_iota(jnp.int32, (8, 1), 0) < 4
        top = jnp.sum(jnp.where(first, lane_row, 0.0), axis=0, keepdims=True)
        low = jnp.sum(jnp.where(first, 0.0, lane_row), axis=0, keepdims=True)
        return jnp.where(first, top, low)

    loads[0].wait()
    density_of(0, vec[...])
    density_arrived(0)
    for tz in range(nz):
        state[:, tz * width : (tz + 1) * width] = dens[0, tz]

    def step(t, carry):
        alpha_row, beta_row = carry
        gath[t, c, a] = state[...].astype(BF16)

        @pl.loop(1, na)
        def _(i):
            ta, device = plane_peer(i)
            pltpu.make_async_remote_copy(
                gath.at[t, c, a], gath.at[t, c, a], gath_send.at[t, ta], gath_recv.at[t, a],
                device, device_id_type=MESH,
            ).start()

        def forward(ta):
            return pltpu.make_async_remote_copy(
                gath.at[t, c, ta], gath.at[t, c, ta], fwd_send.at[t, ta], fwd_recv.at[t, ta],
                partner, device_id_type=MESH,
            )

        forward(a).start()

        @pl.loop(1, na)
        def _(i):
            ta = plane_source(i)
            arrived(gath.at[t, c, ta], gath_recv.at[t, ta])
            forward(ta).start()

        @pl.when(t == 0)
        def _():
            for copy in loads[2:]:
                copy.wait()

        def half_images(h, first):
            wide = gath[t, h].astype(F32)
            rows[...] = wide.reshape(nr, nz * width).astype(BF16)
            for q in range(nq):
                out = lax.dot_general(
                    rows[...], screened_v[h, q], NT, preferred_element_type=F32
                )
                images[q] = out if first else images[q] + out

        half_images(c, True)

        @pl.loop(0, na)
        def _(ta):
            arrived(gath.at[t, other, ta], fwd_recv.at[t, ta])

        half_images(other, False)

        values = images[...].reshape(nq * nr, width)
        high = values.astype(BF16)
        low = (values - high.astype(F32)).astype(BF16)
        chosen = jnp.dot(selector[...], high, preferred_element_type=F32)
        chosen = chosen + jnp.dot(selector[...], low, preferred_element_type=F32)
        field[t] = chosen.reshape(na, 8, width)

        @pl.loop(1, na)
        def _(i):
            ta, device = plane_peer(i)
            pltpu.make_async_remote_copy(
                field.at[t, ta], field_in.at[t, a], field_send.at[t, ta], field_recv.at[t, a],
                device, device_id_type=MESH,
            ).start()

        field_in[t, a] = field[t, a]

        @pl.loop(1, na)
        def _(i):
            ta = plane_source(i)
            arrived(field_in.at[t, ta], field_recv.at[t, ta])

        potential = jnp.sum(field_in[t], axis=0).astype(BF16)

        @pl.when(t == 0)
        def _():
            loads[1].wait()

        partial = jnp.zeros((8, bands), F32)
        for k in range(4):
            out = lax.dot_general(potential, left_v[k], NT, preferred_element_type=F32)
            partial = partial + jnp.where(own_k(bands, k), out, 0.0)
        half_out[t, 0] = partial[:, :half]
        half_out[t, 1] = partial[:, half:]
        pair = pltpu.make_async_remote_copy(
            half_out.at[t, other], half_in.at[t], pair_send.at[t], pair_recv.at[t],
            partner, device_id_type=MESH,
        )
        pair.start()
        arrived(half_in.at[t], pair_recv.at[t])
        direct_z[t, z] = half_out[t, c] + half_in[t]

        @pl.loop(1, nz)
        def _(i):
            tz, device = z_peer(i)
            pltpu.make_async_remote_copy(
                direct_z.at[t, z], direct_z.at[t, z], dz_send.at[t, tz], dz_recv.at[t, z],
                device, device_id_type=MESH,
            ).start()

        @pl.loop(1, nz)
        def _(i):
            tz, _d = z_peer(i)
            arrived(direct_z.at[t, tz], dz_recv.at[t, tz])

        direct_c[t, c] = jnp.sum(direct_z[t], axis=0)
        whole = pltpu.make_async_remote_copy(
            direct_c.at[t, c], direct_c.at[t, c], dc_send.at[t], dc_recv.at[t],
            partner, device_id_type=MESH,
        )
        whole.start()
        arrived(direct_c.at[t, other], dc_recv.at[t])
        direct = jnp.concatenate([direct_c[t, 0], direct_c[t, 1]], axis=1)

        vector = vec[...]
        applied = levels[...] * vector - direct - beta[:, 0:1] * old[...]
        cross = jnp.sum(vector * applied, axis=1, keepdims=True)
        square = jnp.sum(applied * applied, axis=1, keepdims=True)
        norm = jnp.sum(vector * vector, axis=1, keepdims=True)
        sums[t, a] = jnp.where(lane == 0, cross, jnp.where(lane == 1, square, norm))

        @pl.loop(1, na)
        def _(i):
            ta, device = plane_peer(i)
            pltpu.make_async_remote_copy(
                sums.at[t, a], sums.at[t, a], sums_send.at[t, ta], sums_recv.at[t, a],
                device, device_id_type=MESH,
            ).start()

        @pl.when(t < STEPS - 1)
        def _():
            density_of(t + 1, applied)

        @pl.loop(1, na)
        def _(i):
            ta = plane_source(i)
            arrived(sums.at[t, ta], sums_recv.at[t, ta])

        total = jnp.sum(sums[t], axis=0)
        cross_mean = per_row(total, 0) / entries
        square_mean = per_row(total, 1) / entries
        norm_mean = per_row(total, 2) / entries
        alpha = cross_mean
        mean_square = square_mean - 2.0 * alpha * cross_mean + alpha * alpha * norm_mean
        scale = jnp.sqrt(jnp.maximum(mean_square, 0.0) + epsilon)
        old[...] = vector
        vec[...] = (applied - alpha * vector) / scale
        beta[...] = jnp.broadcast_to(scale, (8, 128))

        @pl.when(t < STEPS - 1)
        def _():
            density_arrived(t + 1)
            for tz in range(nz):
                at = slice(tz * width, (tz + 1) * width)
                state[:, at] = (dens[t + 1, tz] - alpha * state[:, at]) / scale

        return jnp.where(lane == t, alpha, alpha_row), jnp.where(lane == t, scale, beta_row)

    zero = jnp.zeros((8, 128), F32)
    alpha_row, beta_row = lax.fori_loop(0, STEPS, step, (zero, zero))
    for tile, ref in ((alpha_row, alphas), (beta_row, betas)):
        ref[0:1, :] = tile[0:1, :STEPS]
        ref[1:2, :] = tile[4:5, :STEPS]
    group = pl.ds(pl.multiple_of((b // 4) * 128, 128), 128)
    for source, ref in ((vec, last), (old, prior)):
        turned = pltpu.roll(source[:, group], lax.rem(128 - lax.rem(b, 4) * 32, 128), 1)
        ref[...] = turned[:, :32]

    def sent(ref, sem):
        pltpu.make_async_copy(ref, ref, sem).wait()

    @pl.loop(1, nz * 2)
    def _(i):
        sent(pk.at[b], pk_send.at[pw_peer(i)[0]])

    @pl.loop(0, STEPS)
    def _(t):
        @pl.loop(1, na)
        def _(i):
            ta = plane_peer(i)[0]
            sent(gath.at[t, c, a], gath_send.at[t, ta])
            sent(field.at[t, ta], field_send.at[t, ta])
            sent(sums.at[t, a], sums_send.at[t, ta])

        @pl.loop(0, na)
        def _(ta):
            sent(gath.at[t, c, ta], fwd_send.at[t, ta])

        @pl.loop(1, nz)
        def _(i):
            tz = z_peer(i)[0]
            sent(dens.at[t, z], dens_send.at[t, tz])
            sent(direct_z.at[t, z], dz_send.at[t, tz])

        sent(half_out.at[t, other], pair_send.at[t])
        sent(direct_c.at[t, c], dc_send.at[t])


def on_device(
    energies, current, previous, previous_beta, pair_left, pair_right, screened, momentum_index
):
    ny, nx, nz = lax.axis_size("kpt_0"), lax.axis_size("kpt_1"), lax.axis_size("pw_0")
    na = ny * nx
    nvec, own_k, own_c = current.shape
    rows = nvec * own_k
    bands, width = pair_left.shape[1:]
    nq = screened.shape[0]
    pack = jnp.concatenate(
        [
            current.reshape(rows, own_c),
            previous.reshape(rows, own_c),
            jnp.concatenate([energies, energies], axis=0),
            jnp.broadcast_to(previous_beta[:, None, None], current.shape).reshape(rows, own_c),
        ],
        axis=1,
    )
    dma = pltpu.SemaphoreType.DMA
    vmem = pl.BlockSpec(memory_space=pltpu.VMEM)
    hbm = pl.BlockSpec(memory_space=pl.ANY)
    last, prior, alphas, betas = pl.pallas_call(
        functools.partial(kernel, (ny, nx, nz)),
        out_shape=(
            jax.ShapeDtypeStruct((rows, own_c), F32),
            jax.ShapeDtypeStruct((rows, own_c), F32),
            jax.ShapeDtypeStruct((nvec, STEPS), F32),
            jax.ShapeDtypeStruct((nvec, STEPS), F32),
        ),
        in_specs=[vmem, vmem, hbm, hbm, hbm],
        out_specs=(vmem, vmem, vmem, vmem),
        scratch_shapes=[
            pltpu.VMEM(pair_left.shape, BF16),
            pltpu.VMEM(pair_right.shape, BF16),
            pltpu.VMEM((2, nq, width, nz * width), BF16),
            pltpu.VMEM((na * 8, nq * na * 8), BF16),
            pltpu.VMEM((nz * 2, 8, 128), F32),
            pltpu.VMEM((STEPS, nz, 8, width), F32),
            pltpu.VMEM((STEPS, 2, na, 8, nz * width), BF16),
            pltpu.VMEM((na * 8, nz * width), BF16),
            pltpu.VMEM((nq, na * 8, width), F32),
            pltpu.VMEM((STEPS, na, 8, width), F32),
            pltpu.VMEM((STEPS, na, 8, width), F32),
            pltpu.VMEM((STEPS, 2, 8, bands // 2), F32),
            pltpu.VMEM((STEPS, 8, bands // 2), F32),
            pltpu.VMEM((STEPS, nz, 8, bands // 2), F32),
            pltpu.VMEM((STEPS, 2, 8, bands // 2), F32),
            pltpu.VMEM((STEPS, na, 8, 128), F32),
            pltpu.VMEM((8, bands), F32),
            pltpu.VMEM((8, bands), F32),
            pltpu.VMEM((8, bands), F32),
            pltpu.VMEM((8, 128), F32),
            pltpu.VMEM((8, nz * width), F32),
            dma((2 + 2 * nz,)),
            dma((nz * 2,)),
            dma((nz * 2,)),
            dma((STEPS, nz)),
            dma((STEPS, nz)),
            dma((STEPS, na)),
            dma((STEPS, na)),
            dma((STEPS, na)),
            dma((STEPS, na)),
            dma((STEPS, na)),
            dma((STEPS, na)),
            dma((STEPS,)),
            dma((STEPS,)),
            dma((STEPS, nz)),
            dma((STEPS, nz)),
            dma((STEPS,)),
            dma((STEPS,)),
            dma((STEPS, na)),
            dma((STEPS, na)),
        ],
        compiler_params=pltpu.CompilerParams(
            collective_id=0, has_side_effects=True, vmem_limit_bytes=60 * 1024 * 1024
        ),
    )(pack, momentum_index, pair_left, pair_right, screened)
    return last.reshape(current.shape), prior.reshape(current.shape), alphas, betas


def solution(mesh):
    kpt, pw = mesh.devices.shape
    ny = 4 if kpt % 4 == 0 else kpt
    finer = Mesh(
        mesh.devices.reshape(ny, kpt // ny, pw // 2, 2), ("kpt_0", "kpt_1", "pw_0", "pw_1")
    )
    in_specs = (
        P(KPT, PW),
        P(None, KPT, PW),
        P(None, KPT, PW),
        P(),
        P(KPT, None, PW),
        P(KPT, None, PW),
        P(KPT, PW, None),
        P(),
    )
    out_specs = (P(None, KPT, PW), P(None, KPT, PW), P(), P())
    return jax.shard_map(
        on_device, mesh=finer, in_specs=in_specs, out_specs=out_specs, check_vma=False
    )
```

time: 375 us -> 125 us (0.33)
  blocking collectives: 286 us -> 0 us
  Pallas kernels: 0 us -> 116 us
  waiting for transfers between devices: 39.5 us -> 0 us
  matrix products: 23 us -> 0 us
  starting transfers between devices: 10.2 us -> 0 us
  local copies, waits for them, and re-layouts: 11.6 us -> 5.83 us
    all_to_all x10 -> x0, blocking collectives: 162 us -> none  [the longest x7 133 us: sent_to_all(): return lax.all_to_all(copies, axis, split_axis=0, concat_axis=0, tiled=True)]
    pallas_call x0 -> x1, Pallas kernels: none -> 116 us  [on_device(): pl.pallas_call(functools.partial(kernel, (ny, nx, nz)), out_shape=(jax.Sh...]
    psum x12 -> x0, blocking collectives: 102 us -> none  [over_axes(): return functools.reduce(lax.psum, axes, x)]
    all_to_all x2 -> x0, waiting for transfers between devices: 39.5 us -> none  [sent_to_all(): return lax.all_to_all(copies, axis, split_axis=0, concat_axis=0, tiled=True)]
    dot_general x12 -> x0, matrix products: 23 us -> none  [the longest x3 18.8 us: screened_images(): jnp.einsum('qsg,kvg->qkvs', screened, collect(kpoint_rows, PW, 2), prefer...]
    all_gather x1 -> x0, blocking collectives: 21.8 us -> none  [rows_first(): out, at, done = (lax.all_gather(both, axis, axis=0, tiled=True), 0, [])]
    all_to_all x2 -> x0, starting transfers between devices: 10.2 us -> none  [sent_to_all(): return lax.all_to_all(copies, axis, split_axis=0, concat_axis=0, tiled=True)]
    reshape x14 -> x0, local copies, waits for them, and re-layouts: 3.92 us -> none  [the longest x6 3.75 us: laid_out(): return jnp.moveaxis(blocks, 0, dim).reshape(lengths)]
  transfers between devices with their start and end apart: 2 -> 0, of which waited for: 2 -> 0; matrix products, arithmetic and copies ran while one was open for 0% -> 0% of each run, Pallas kernels for 0% -> 0%
where the time goes in v1:
time: 125 us; the launch traced here: 124 us
  Pallas kernels  116 us (93%)
  local copies, waits for them, and re-layouts  5.83 us (5%)
  other arithmetic  1.43 us (1%)
    pallas_call x1, Pallas kernels, on_device(): pl.pallas_call(functools.partial(kernel, (ny, nx, nz)), out_shape=(jax.Sh...  116 us
    unnamed x4, local copies, waits for them, and re-layouts  4.95 us

profile of v1, /device:TPU:1, one launch (start us, length us, event | category | flops | bytes accessed | tf_op | source)
XLA Modules:
  0.0 124.3 jit_solution(3909013884406812622)
XLA Ops:
  0.6 0.7 broadcast_in_dim.10
  1.4 0.1 broadcast_in_dim.11
  1.4 0.1 broadcast_in_dim.12
  1.5 1.4 %pad_maximum_fusion.pack = f32[8,128]{1,0:T(8,128)} fusion(f32[8,32]{1,0:T(8,128)S(1)} %broadcast_in_dim.12, f32[4,32]{1,0:T(4,128)} %param.8, f32[8,32]{1,0:T(8,128)} %bitcast.6, f32[8,32]{1,0:T(8,128)} %bitcast.7), kind=kLoop, calls=%fused_computation | loop fusion | flops 4096 | bytes 7680 | tf_op jit(solution)/shard_map/concatenate | solution.py:384
  2.9 116.3 %shard_map.111 = (f32[8,32]{1,0:T(8,128)}, f32[8,32]{1,0:T(8,128)}, f32[2,3]{1,0:T(2,128)}, f32[2,3]{1,0:T(2,128)}) custom-call(f32[8,128]{1,0:T(8,128)} %pad_maximum_fusion.pack, s32[64,64]{1,0:T(8,128)} %momentum.1, bf16[4,512,256]{2,1,0:T(8,128)(2,1)} %left.1, bf16[4,512,256]{2,1,0:T(8,128)(2,1)} %right.1, bf16[4,256,4096]{2,1,0:T(8,128)(2,1)} %screened.1), custom_call_target="tpu_custom_call" | custom-call | tf_op jit(solution)/shard_map/pallas_call | solution.py:396
  119.3 1.3 %copy.16 = f32[2,4,32]{2,1,0:T(4,128)} copy(f32[2,4,32]{2,1,0:T(4,128)} %bitcast.5) | data formatting | bytes 2048
  120.6 1.3 %copy.17 = f32[2,4,32]{2,1,0:T(4,128)} copy(f32[2,4,32]{2,1,0:T(4,128)} %bitcast.4) | data formatting | bytes 2048
  121.8 1.2 copy.18
  123.1 1.2 copy.19

commit v2 on v1

--- a/solution.py
+++ b/solution.py
@@ -20,12 +20,13 @@
 
 
 def kernel(
-    sizes, pack, momentum, left, right, screened,
-    last, prior, alphas, betas,
+    sizes, energies, current, previous, first_beta, momentum_h, left, right, screened,
+    packed,
+    energies_v, current_v, previous_v, first_beta_s, momentum,
     left_v, right_v, screened_v, selector,
-    pk, dens, gath, rows, images, field, field_in, half_out, half_in, direct_z, direct_c, sums,
-    vec, old, levels, beta, state,
-    load_sem, pk_send, pk_recv, dens_send, dens_recv, gath_send, gath_recv, fwd_send, fwd_recv,
+    pk, gath, gained, images, field, field_in, half_out, half_in, direct_z, direct_c, sums,
+    vec, old, levels, beta, applied_v,
+    small_sem, load_sem, pk_send, pk_recv, gz_send, gz_recv, gx_send, gx_recv, fwd_send, fwd_recv,
     field_send, field_recv, pair_send, pair_recv, dz_send, dz_recv, dc_send, dc_recv,
     sums_send, sums_recv,
 ):
@@ -55,12 +56,28 @@
         tz = lax.rem(z + i, nz)
         return tz, (y, x, tz, c)
 
+    def z_near(i):
+        far, odd = (i + 1) // 2, lax.rem(i, 2)
+        return lax.rem(z + odd * far + (1 - odd) * (nz - far), nz)
+
     def pw_peer(i):
         t = lax.rem(b + i, nz * 2)
         return t, (y, x, t // 2, lax.rem(t, 2))
 
     partner = (y, x, z, other)
 
+    small = [
+        pltpu.make_async_copy(source, target, small_sem.at[n])
+        for n, (source, target) in enumerate(
+            (
+                (current, current_v),
+                (previous, previous_v),
+                (energies, energies_v),
+                (first_beta, first_beta_s),
+                (momentum_h, momentum),
+            )
+        )
+    ]
     loads = [
         pltpu.make_async_copy(right, right_v, load_sem.at[0]),
         pltpu.make_async_copy(left, left_v, load_sem.at[1]),
@@ -71,11 +88,11 @@
             loads.append(
                 pltpu.make_async_copy(
                     screened.at[:, :, pl.ds(at, width)],
-                    screened_v.at[h, :, :, pl.ds(t * width, width)],
+                    screened_v.at[h, t],
                     load_sem.at[2 + h * nz + t],
                 )
             )
-    for copy in loads:
+    for copy in small + loads:
         copy.start()
 
     barrier = pltpu.get_barrier_semaphore()
@@ -87,6 +104,14 @@
     @pl.loop(1, nz * 2)
     def _(i):
         pl.semaphore_signal(barrier, inc=1, device_id=pw_peer(i)[1], device_id_type=MESH)
+
+    for copy in small:
+        copy.wait()
+    blank = jnp.zeros((4, 32), F32)
+    for n in range(2):
+        pk[b, n * 4 : n * 4 + 4, :] = jnp.concatenate(
+            [current_v[n], previous_v[n], energies_v[...], blank], axis=1
+        )
 
     nr = na * 8
     nk = momentum.shape[0]
@@ -103,7 +128,6 @@
         hit = jnp.logical_and(by_both == a * nq + q, same)
         selector[:, q * nr : (q + 1) * nr] = jnp.where(hit, 1.0, 0.0).astype(BF16)
 
-    pk[b] = pack[...]
     pl.semaphore_wait(barrier, na - 1 + nz * 2 - 1)
 
     def pk_copy(i):
@@ -135,94 +159,129 @@
                     turned = pltpu.roll(turned, shift, 1)
                 total = total + jnp.where(lane // 32 == m, turned, 0.0)
             ref[:, j * 128 : (j + 1) * 128] = total
-    beta[...] = jnp.broadcast_to(pack[:, 96:97], (8, 128))
+    upper = lax.broadcasted_iota(jnp.int32, (8, 128), 0) < 4
+    beta[...] = jnp.where(upper, first_beta_s[0], first_beta_s[1])
 
     def own_k(n, k):
         return lax.broadcasted_iota(jnp.int32, (8, n), 0) % 4 == k
 
-    def density_of(t, values):
+    def row_total(column):
+        first = lax.broadcasted_iota(jnp.int32, (8, 1), 0) < 4
+        top = jnp.sum(jnp.where(first, column, 0.0), axis=0, keepdims=True)
+        low = jnp.sum(jnp.where(first, 0.0, column), axis=0, keepdims=True)
+        return jnp.where(first, top, low)
+
+    def share(cross, norm):
+        some = norm > 1e-30
+        return jnp.where(some, cross / jnp.where(some, norm, 1.0), 0.0)
+
+    def to_plane(t, tz):
+        @pl.loop(1, na)
+        def _(i):
+            pltpu.make_async_remote_copy(
+                gath.at[t, c, tz, a], gath.at[t, c, tz, a], gx_send.at[t, tz], gx_recv.at[t, tz],
+                plane_peer(i)[1], device_id_type=MESH,
+            ).start()
+
+    def send_density(t, values):
         high = values.astype(BF16).astype(F32)
         both = jnp.concatenate([high, values - high], axis=0).astype(BF16)
         total = jnp.zeros((8, width), F32)
         for k in range(4):
             out = jnp.dot(both, right_v[k], preferred_element_type=F32)
             total = total + jnp.where(own_k(width, k), out[0:8] + out[8:16], 0.0)
-        dens[t, z] = total
+        gath[t, c, z, a] = total.astype(BF16)
 
         @pl.loop(1, nz)
         def _(i):
-            tz, device = z_peer(i)
+            tz = z_near(nz - i)
             pltpu.make_async_remote_copy(
-                dens.at[t, z], dens.at[t, z], dens_send.at[t, tz], dens_recv.at[t, z],
-                device, device_id_type=MESH,
+                gath.at[t, c, z, a], gath.at[t, c, z, a], gz_send.at[t, tz], gz_recv.at[t, z],
+                (y, x, tz, c), device_id_type=MESH,
             ).start()
 
-    def density_arrived(t):
+        to_plane(t, z)
+
+    def gain(t, h, tz, first):
+        block = gath[t, h, tz].astype(F32).reshape(nr, width).astype(BF16)
+        for q in range(nq):
+            out = lax.dot_general(block, screened_v[h, tz, q], NT, preferred_element_type=F32)
+            gained[q] = out if first else gained[q] + out
+
+    def finish(t, with_images):
+        @pl.loop(1, na)
+        def _(i):
+            ta = plane_source(i)
+            arrived(sums.at[t, ta], sums_recv.at[t, ta])
+
+        total = jnp.sum(sums[t], axis=0)
+        cross_mean = total[:, 0:1] / entries
+        square_mean = total[:, 1:2] / entries
+        norm_mean = total[:, 2:3] / entries
+        alpha = cross_mean
+        mean_square = square_mean - 2.0 * alpha * cross_mean + alpha * alpha * norm_mean
+        scale = jnp.sqrt(jnp.maximum(mean_square, 0.0) + epsilon)
+        vector = vec[...]
+        old[...] = vector
+        vec[...] = (applied_v[...] - alpha * vector) / scale
+        beta[...] = jnp.broadcast_to(scale, (8, 128))
+        packed[2] = jnp.where(lane == t, alpha, packed[2])
+        packed[3] = jnp.where(lane == t, scale, packed[3])
+        if with_images:
+            every = sums[t].reshape(nr, 128)
+            rest = jnp.broadcast_to(alpha[None], (na, 8, 128)).reshape(nr, 128)[:, 0:1]
+            rest = rest - share(every[:, 0:1], every[:, 2:3])
+            inverse = jnp.broadcast_to((1.0 / scale)[None], (na, 8, 128)).reshape(nr, 128)[:, 0:1]
+            for q in range(nq):
+                images[q] = (gained[q] - rest * images[q]) * inverse
+
+    packed[2] = jnp.zeros((8, 128), F32)
+    packed[3] = jnp.zeros((8, 128), F32)
+    loads[0].wait()
+    send_density(0, vec[...])
+
+    @pl.loop(0, STEPS)
+    def _(t):
         @pl.loop(1, nz)
         def _(i):
-            tz, _d = z_peer(i)
-            arrived(dens.at[t, tz], dens_recv.at[t, tz])
-
-    def per_row(tile, at):
-        lane_row = tile[:, at : at + 1]
-        first = lax.broadcasted_iota(jnp.int32, (8, 1), 0) < 4
-        top = jnp.sum(jnp.where(first, lane_row, 0.0), axis=0, keepdims=True)
-        low = jnp.sum(jnp.where(first, 0.0, lane_row), axis=0, keepdims=True)
-        return jnp.where(first, top, low)
-
-    loads[0].wait()
-    density_of(0, vec[...])
-    density_arrived(0)
-    for tz in range(nz):
-        state[:, tz * width : (tz + 1) * width] = dens[0, tz]
-
-    def step(t, carry):
-        alpha_row, beta_row = carry
-        gath[t, c, a] = state[...].astype(BF16)
-
-        @pl.loop(1, na)
-        def _(i):
-            ta, device = plane_peer(i)
-            pltpu.make_async_remote_copy(
-                gath.at[t, c, a], gath.at[t, c, a], gath_send.at[t, ta], gath_recv.at[t, a],
-                device, device_id_type=MESH,
-            ).start()
-
-        def forward(ta):
-            return pltpu.make_async_remote_copy(
-                gath.at[t, c, ta], gath.at[t, c, ta], fwd_send.at[t, ta], fwd_recv.at[t, ta],
-                partner, device_id_type=MESH,
-            )
-
-        forward(a).start()
-
-        @pl.loop(1, na)
-        def _(i):
-            ta = plane_source(i)
-            arrived(gath.at[t, c, ta], gath_recv.at[t, ta])
-            forward(ta).start()
+            tz = z_near(i)
+            arrived(gath.at[t, c, tz, a], gz_recv.at[t, tz])
+            to_plane(t, tz)
 
         @pl.when(t == 0)
         def _():
             for copy in loads[2:]:
                 copy.wait()
 
-        def half_images(h, first):
-            wide = gath[t, h].astype(F32)
-            rows[...] = wide.reshape(nr, nz * width).astype(BF16)
-            for q in range(nq):
-                out = lax.dot_general(
-                    rows[...], screened_v[h, q], NT, preferred_element_type=F32
-                )
-                images[q] = out if first else images[q] + out
-
-        half_images(c, True)
-
-        @pl.loop(0, na)
-        def _(ta):
-            arrived(gath.at[t, other, ta], fwd_recv.at[t, ta])
-
-        half_images(other, False)
+        def forward(tz):
+            arrived(gath.at[t, c, tz, pl.ds(0, na - 1)], gx_recv.at[t, tz])
+            pltpu.make_async_remote_copy(
+                gath.at[t, c, tz], gath.at[t, c, tz], fwd_send.at[t, tz], fwd_recv.at[t, tz],
+                partner, device_id_type=MESH,
+            ).start()
+
+        forward(z)
+        gain(t, c, z, True)
+
+        @pl.loop(1, nz)
+        def _(i):
+            tz = z_near(i)
+            forward(tz)
+            gain(t, c, tz, False)
+
+        @pl.loop(0, nz)
+        def _(i):
+            tz = z_near(i)
+            arrived(gath.at[t, other, tz], fwd_recv.at[t, tz])
+            gain(t, other, tz, False)
+
+        @pl.when(t == 0)
+        def _():
+            images[...] = gained[...]
+
+        @pl.when(t > 0)
+        def _():
+            finish(t - 1, True)
 
         values = images[...].reshape(nq * nr, width)
         high = values.astype(BF16)
@@ -293,7 +352,13 @@
         cross = jnp.sum(vector * applied, axis=1, keepdims=True)
         square = jnp.sum(applied * applied, axis=1, keepdims=True)
         norm = jnp.sum(vector * vector, axis=1, keepdims=True)
+        cross, square, norm = row_total(cross), row_total(square), row_total(norm)
         sums[t, a] = jnp.where(lane == 0, cross, jnp.where(lane == 1, square, norm))
+        applied_v[...] = applied
+
+        @pl.when(t < STEPS - 1)
+        def _():
+            send_density(t + 1, applied - share(cross, norm) * vector)
 
         @pl.loop(1, na)
         def _(i):
@@ -303,44 +368,10 @@
                 device, device_id_type=MESH,
             ).start()
 
-        @pl.when(t < STEPS - 1)
-        def _():
-            density_of(t + 1, applied)
-
-        @pl.loop(1, na)
-        def _(i):
-            ta = plane_source(i)
-            arrived(sums.at[t, ta], sums_recv.at[t, ta])
-
-        total = jnp.sum(sums[t], axis=0)
-        cross_mean = per_row(total, 0) / entries
-        square_mean = per_row(total, 1) / entries
-        norm_mean = per_row(total, 2) / entries
-        alpha = cross_mean
-        mean_square = square_mean - 2.0 * alpha * cross_mean + alpha * alpha * norm_mean
-        scale = jnp.sqrt(jnp.maximum(mean_square, 0.0) + epsilon)
-        old[...] = vector
-        vec[...] = (applied - alpha * vector) / scale
-        beta[...] = jnp.broadcast_to(scale, (8, 128))
-
-        @pl.when(t < STEPS - 1)
-        def _():
-            density_arrived(t + 1)
-            for tz in range(nz):
-                at = slice(tz * width, (tz + 1) * width)
-                state[:, at] = (dens[t + 1, tz] - alpha * state[:, at]) / scale
-
-        return jnp.where(lane == t, alpha, alpha_row), jnp.where(lane == t, scale, beta_row)
-
-    zero = jnp.zeros((8, 128), F32)
-    alpha_row, beta_row = lax.fori_loop(0, STEPS, step, (zero, zero))
-    for tile, ref in ((alpha_row, alphas), (beta_row, betas)):
-        ref[0:1, :] = tile[0:1, :STEPS]
-        ref[1:2, :] = tile[4:5, :STEPS]
+    finish(STEPS - 1, False)
     group = pl.ds(pl.multiple_of((b // 4) * 128, 128), 128)
-    for source, ref in ((vec, last), (old, prior)):
-        turned = pltpu.roll(source[:, group], lax.rem(128 - lax.rem(b, 4) * 32, 128), 1)
-        ref[...] = turned[:, :32]
+    for n, source in enumerate((vec, old)):
+        packed[n] = pltpu.roll(source[:, group], lax.rem(128 - lax.rem(b, 4) * 32, 128), 1)
 
     def sent(ref, sem):
         pltpu.make_async_copy(ref, ref, sem).wait()
@@ -354,22 +385,31 @@
         @pl.loop(1, na)
         def _(i):
             ta = plane_peer(i)[0]
-            sent(gath.at[t, c, a], gath_send.at[t, ta])
             sent(field.at[t, ta], field_send.at[t, ta])
             sent(sums.at[t, a], sums_send.at[t, ta])
 
-        @pl.loop(0, na)
-        def _(ta):
-            sent(gath.at[t, c, ta], fwd_send.at[t, ta])
+        @pl.loop(0, nz)
+        def _(tz):
+            sent(gath.at[t, c, tz, pl.ds(0, na - 1)], gx_send.at[t, tz])
+            sent(gath.at[t, c, tz], fwd_send.at[t, tz])
 
         @pl.loop(1, nz)
         def _(i):
             tz = z_peer(i)[0]
-            sent(dens.at[t, z], dens_send.at[t, tz])
+            sent(gath.at[t, c, z, a], gz_send.at[t, tz])
             sent(direct_z.at[t, z], dz_send.at[t, tz])
 
         sent(half_out.at[t, other], pair_send.at[t])
         sent(direct_c.at[t, c], dc_send.at[t])
+
+
+def unpack(packed, last, prior, alphas, betas):
+    for n, ref in ((0, last), (1, prior)):
+        ref[0] = packed[n, 0:4, :32]
+        ref[1] = packed[n, 4:8, :32]
+    for n, ref in ((2, alphas), (3, betas)):
+        ref[0:1, :] = packed[n, 0:1, :STEPS]
+        ref[1:2, :] = packed[n, 4:5, :STEPS]
 
 
 def on_device(
@@ -377,41 +417,30 @@
 ):
     ny, nx, nz = lax.axis_size("kpt_0"), lax.axis_size("kpt_1"), lax.axis_size("pw_0")
     na = ny * nx
-    nvec, own_k, own_c = current.shape
-    rows = nvec * own_k
+    nvec = current.shape[0]
     bands, width = pair_left.shape[1:]
     nq = screened.shape[0]
-    pack = jnp.concatenate(
-        [
-            current.reshape(rows, own_c),
-            previous.reshape(rows, own_c),
-            jnp.concatenate([energies, energies], axis=0),
-            jnp.broadcast_to(previous_beta[:, None, None], current.shape).reshape(rows, own_c),
-        ],
-        axis=1,
-    )
     dma = pltpu.SemaphoreType.DMA
     vmem = pl.BlockSpec(memory_space=pltpu.VMEM)
     hbm = pl.BlockSpec(memory_space=pl.ANY)
-    last, prior, alphas, betas = pl.pallas_call(
+    packed = pl.pallas_call(
         functools.partial(kernel, (ny, nx, nz)),
-        out_shape=(
-            jax.ShapeDtypeStruct((rows, own_c), F32),
-            jax.ShapeDtypeStruct((rows, own_c), F32),
-            jax.ShapeDtypeStruct((nvec, STEPS), F32),
-            jax.ShapeDtypeStruct((nvec, STEPS), F32),
-        ),
-        in_specs=[vmem, vmem, hbm, hbm, hbm],
-        out_specs=(vmem, vmem, vmem, vmem),
+        out_shape=jax.ShapeDtypeStruct((4, 8, 128), F32),
+        in_specs=[hbm] * 8,
+        out_specs=vmem,
         scratch_shapes=[
+            pltpu.VMEM(energies.shape, F32),
+            pltpu.VMEM(current.shape, F32),
+            pltpu.VMEM(previous.shape, F32),
+            pltpu.SMEM(previous_beta.shape, F32),
+            pltpu.VMEM(momentum_index.shape, jnp.int32),
             pltpu.VMEM(pair_left.shape, BF16),
             pltpu.VMEM(pair_right.shape, BF16),
-            pltpu.VMEM((2, nq, width, nz * width), BF16),
+            pltpu.VMEM((2, nz, nq, width, width), BF16),
             pltpu.VMEM((na * 8, nq * na * 8), BF16),
             pltpu.VMEM((nz * 2, 8, 128), F32),
-            pltpu.VMEM((STEPS, nz, 8, width), F32),
-            pltpu.VMEM((STEPS, 2, na, 8, nz * width), BF16),
-            pltpu.VMEM((na * 8, nz * width), BF16),
+            pltpu.VMEM((STEPS, 2, nz, na, 8, width), BF16),
+            pltpu.VMEM((nq, na * 8, width), F32),
             pltpu.VMEM((nq, na * 8, width), F32),
             pltpu.VMEM((STEPS, na, 8, width), F32),
             pltpu.VMEM((STEPS, na, 8, width), F32),
@@ -424,16 +453,17 @@
             pltpu.VMEM((8, bands), F32),
             pltpu.VMEM((8, bands), F32),
             pltpu.VMEM((8, 128), F32),
-            pltpu.VMEM((8, nz * width), F32),
+            pltpu.VMEM((8, bands), F32),
+            dma((5,)),
             dma((2 + 2 * nz,)),
             dma((nz * 2,)),
             dma((nz * 2,)),
             dma((STEPS, nz)),
             dma((STEPS, nz)),
-            dma((STEPS, na)),
-            dma((STEPS, na)),
-            dma((STEPS, na)),
-            dma((STEPS, na)),
+            dma((STEPS, nz)),
+            dma((STEPS, nz)),
+            dma((STEPS, nz)),
+            dma((STEPS, nz)),
             dma((STEPS, na)),
             dma((STEPS, na)),
             dma((STEPS,)),
@@ -448,8 +478,22 @@
         compiler_params=pltpu.CompilerParams(
             collective_id=0, has_side_effects=True, vmem_limit_bytes=60 * 1024 * 1024
         ),
-    )(pack, momentum_index, pair_left, pair_right, screened)
-    return last.reshape(current.shape), prior.reshape(current.shape), alphas, betas
+    )(
+        energies, current, previous, previous_beta, momentum_index, pair_left, pair_right, screened
+    )
+    return tuple(
+        pl.pallas_call(
+            unpack,
+            out_shape=(
+                jax.ShapeDtypeStruct(current.shape, F32),
+                jax.ShapeDtypeStruct(current.shape, F32),
+                jax.ShapeDtypeStruct((nvec, STEPS), F32),
+                jax.ShapeDtypeStruct((nvec, STEPS), F32),
+            ),
+            in_specs=[vmem],
+            out_specs=(vmem, vmem, vmem, vmem),
+        )(packed)
+    )
 
 
 def solution(mesh):

time: 125 us -> 109 us (0.87)
  Pallas kernels: 116 us -> 109 us
  local copies, waits for them, and re-layouts: 5.83 us -> 0 us
  other arithmetic: 1.43 us -> 0 us
    pallas_call x1 -> x2, Pallas kernels: 116 us -> 109 us  [the longest x1 107 us: on_device(): pl.pallas_call(functools.partial(kernel, (ny, nx, nz)), out_shape=jax.Sha...]
    unnamed x4 -> x0, local copies, waits for them, and re-layouts: 4.95 us -> none
    concatenate x1 -> x0, other arithmetic: 1.43 us -> none  [on_device(): jnp.concatenate([current.reshape(rows, own_c), previous.reshape(rows, own...]
where the time goes in v2:
time: 109 us
  Pallas kernels  109 us (100%)
    pallas_call x1, Pallas kernels, on_device(): pl.pallas_call(functools.partial(kernel, (ny, nx, nz)), out_shape=jax.Sha...  107 us

profile of v2, /device:TPU:1, one launch (start us, length us, event | category | flops | bytes accessed | tf_op | source)
XLA Modules:
  0.0 109.2 jit_solution(11207121632411453594)
XLA Ops:
  0.6 107.2 %shard_map.111.packed = f32[4,8,128]{2,1,0:T(8,128)} custom-call(f32[4,32]{1,0:T(4,128)} %energies.1, f32[2,4,32]{2,1,0:T(4,128)} %current.1, f32[2,4,32]{2,1,0:T(4,128)} %previous.1, f32[2]{0:T(128)} %first_beta.1, s32[64,64]{1,0:T(8,128)} %momentum_h.1, bf16[4,512,256]{2,1,0:T(8,128)(2,1)} %left.1, bf16[4,512,256]{2,1,0:T(8,128)(2,1)} %right.1, ...), custom_call_target="tpu_custom_call" | custom-call | tf_op jit(solution)/shard_map/pallas_call | solution.py:426
  107.9 1.3 %shard_map.112 = (f32[2,4,32]{2,1,0:T(4,128)}, f32[2,4,32]{2,1,0:T(4,128)}, f32[2,3]{1,0:T(2,128)}, f32[2,3]{1,0:T(2,128)}) custom-call(f32[4,8,128]{2,1,0:T(8,128)} %shard_map.111.packed), custom_call_target="tpu_custom_call" | custom-call | tf_op jit(solution)/shard_map/pallas_call | solution.py:485

commit v3 on v2

--- a/solution.py
+++ b/solution.py
@@ -24,11 +24,10 @@
     packed,
     energies_v, current_v, previous_v, first_beta_s, momentum,
     left_v, right_v, screened_v, selector,
-    pk, gath, gained, images, field, field_in, half_out, half_in, direct_z, direct_c, sums,
-    vec, old, levels, beta, applied_v,
+    left_o, pk, gath, gained, images, field, field_in, direct, sums,
+    vec, old, levels, beta, applied_v, rest_v, inverse_v,
     small_sem, load_sem, pk_send, pk_recv, gz_send, gz_recv, gx_send, gx_recv, fwd_send, fwd_recv,
-    field_send, field_recv, pair_send, pair_recv, dz_send, dz_recv, dc_send, dc_recv,
-    sums_send, sums_recv,
+    field_send, field_recv, direct_send, direct_recv, sums_send, sums_recv, left_send, left_recv,
 ):
     ny, nx, nz = sizes
     na = ny * nx
@@ -42,10 +41,16 @@
     a = y * nx + x
     b = z * 2 + c
 
-    def plane_peer(i):
-        ty = lax.rem(y + i // nx, ny)
-        tx = lax.rem(x + lax.rem(i, nx), nx)
-        return ty * nx + tx, (ty, tx, z, c)
+    tys = [lax.rem(y + d, ny) for d in range(ny)]
+    txs = [lax.rem(x + d, nx) for d in range(nx)]
+    far_first = sorted(
+        ((dy, dx) for dy in range(ny) for dx in range(nx) if dy or dx),
+        key=lambda d: -min(d[0], ny - d[0]) - min(d[1], nx - d[1]),
+    )
+
+    def plane_sends(send):
+        for dy, dx in far_first:
+            send(tys[dy] * nx + txs[dx], tys[dy], txs[dx])
 
     def plane_source(i):
         ty = lax.rem(y + ny - i // nx, ny)
@@ -97,13 +102,18 @@
 
     barrier = pltpu.get_barrier_semaphore()
 
-    @pl.loop(1, na)
-    def _(i):
-        pl.semaphore_signal(barrier, inc=1, device_id=plane_peer(i)[1], device_id_type=MESH)
+    def greet(device):
+        pl.semaphore_signal(barrier, inc=1, device_id=device, device_id_type=MESH)
 
     @pl.loop(1, nz * 2)
     def _(i):
-        pl.semaphore_signal(barrier, inc=1, device_id=pw_peer(i)[1], device_id_type=MESH)
+        greet(pw_peer(i)[1])
+
+    def greet_both(ta, ty, tx):
+        greet((ty, tx, z, c))
+        greet((ty, tx, z, other))
+
+    plane_sends(greet_both)
 
     for copy in small:
         copy.wait()
@@ -128,7 +138,12 @@
         hit = jnp.logical_and(by_both == a * nq + q, same)
         selector[:, q * nr : (q + 1) * nr] = jnp.where(hit, 1.0, 0.0).astype(BF16)
 
-    pl.semaphore_wait(barrier, na - 1 + nz * 2 - 1)
+    pl.semaphore_wait(barrier, 2 * (na - 1) + nz * 2 - 1)
+
+    left_copy = pltpu.make_async_remote_copy(
+        left_v.at[:, pl.ds(pl.multiple_of(other * half, half), half), :], left_o,
+        left_send, left_recv, partner, device_id_type=MESH,
+    )
 
     def pk_copy(i):
         t, device = pw_peer(i)
@@ -176,12 +191,13 @@
         return jnp.where(some, cross / jnp.where(some, norm, 1.0), 0.0)
 
     def to_plane(t, tz):
-        @pl.loop(1, na)
-        def _(i):
+        def send(ta, ty, tx):
             pltpu.make_async_remote_copy(
                 gath.at[t, c, tz, a], gath.at[t, c, tz, a], gx_send.at[t, tz], gx_recv.at[t, tz],
-                plane_peer(i)[1], device_id_type=MESH,
+                (ty, tx, z, c), device_id_type=MESH,
             ).start()
+
+        plane_sends(send)
 
     def send_density(t, values):
         high = values.astype(BF16).astype(F32)
@@ -208,12 +224,8 @@
             out = lax.dot_general(block, screened_v[h, tz, q], NT, preferred_element_type=F32)
             gained[q] = out if first else gained[q] + out
 
-    def finish(t, with_images):
-        @pl.loop(1, na)
-        def _(i):
-            ta = plane_source(i)
-            arrived(sums.at[t, ta], sums_recv.at[t, ta])
-
+    def finish(t):
+        arrived(sums.at[t, pl.ds(0, na - 1)], sums_recv.at[t])
         total = jnp.sum(sums[t], axis=0)
         cross_mean = total[:, 0:1] / entries
         square_mean = total[:, 1:2] / entries
@@ -227,18 +239,20 @@
         beta[...] = jnp.broadcast_to(scale, (8, 128))
         packed[2] = jnp.where(lane == t, alpha, packed[2])
         packed[3] = jnp.where(lane == t, scale, packed[3])
-        if with_images:
-            every = sums[t].reshape(nr, 128)
-            rest = jnp.broadcast_to(alpha[None], (na, 8, 128)).reshape(nr, 128)[:, 0:1]
-            rest = rest - share(every[:, 0:1], every[:, 2:3])
-            inverse = jnp.broadcast_to((1.0 / scale)[None], (na, 8, 128)).reshape(nr, 128)[:, 0:1]
-            for q in range(nq):
-                images[q] = (gained[q] - rest * images[q]) * inverse
+        every = sums[t].reshape(nr, 128)
+        rest = jnp.broadcast_to(alpha[None], (na, 8, 128)).reshape(nr, 128)
+        rest_v[...] = rest - share(every[:, 0:1], every[:, 2:3])
+        inverse_v[...] = jnp.broadcast_to((1.0 / scale)[None], (na, 8, 128)).reshape(nr, 128)
 
     packed[2] = jnp.zeros((8, 128), F32)
     packed[3] = jnp.zeros((8, 128), F32)
+    rest_v[...] = jnp.zeros_like(rest_v)
+    inverse_v[...] = jnp.ones_like(inverse_v)
+    images[...] = jnp.zeros_like(images)
     loads[0].wait()
     send_density(0, vec[...])
+    loads[1].wait()
+    left_copy.start()
 
     @pl.loop(0, STEPS)
     def _(t):
@@ -269,86 +283,82 @@
             forward(tz)
             gain(t, c, tz, False)
 
+        @pl.when(t > 0)
+        def _():
+            finish(t - 1)
+
         @pl.loop(0, nz)
         def _(i):
             tz = z_near(i)
             arrived(gath.at[t, other, tz], fwd_recv.at[t, tz])
             gain(t, other, tz, False)
 
-        @pl.when(t == 0)
-        def _():
-            images[...] = gained[...]
-
-        @pl.when(t > 0)
-        def _():
-            finish(t - 1, True)
+        rest, inverse = rest_v[:, 0:1], inverse_v[:, 0:1]
+        for q in range(nq):
+            images[q] = (gained[q] - rest * images[q]) * inverse
 
         values = images[...].reshape(nq * nr, width)
         high = values.astype(BF16)
         low = (values - high.astype(F32)).astype(BF16)
         chosen = jnp.dot(selector[...], high, preferred_element_type=F32)
         chosen = chosen + jnp.dot(selector[...], low, preferred_element_type=F32)
-        field[t] = chosen.reshape(na, 8, width)
-
-        @pl.loop(1, na)
-        def _(i):
-            ta, device = plane_peer(i)
-            pltpu.make_async_remote_copy(
-                field.at[t, ta], field_in.at[t, a], field_send.at[t, ta], field_recv.at[t, a],
-                device, device_id_type=MESH,
-            ).start()
-
-        field_in[t, a] = field[t, a]
-
-        @pl.loop(1, na)
-        def _(i):
-            ta = plane_source(i)
-            arrived(field_in.at[t, ta], field_recv.at[t, ta])
-
-        potential = jnp.sum(field_in[t], axis=0).astype(BF16)
+        field[t] = chosen.reshape(na, 8, width).astype(BF16)
+
+        def send_field(ta, ty, tx):
+            for n, core in enumerate((c, other)):
+                pltpu.make_async_remote_copy(
+                    field.at[t, ta], field_in.at[t, c, a], field_send.at[t, n],
+                    field_recv.at[t, c], (ty, tx, z, core), device_id_type=MESH,
+                ).start()
+
+        plane_sends(send_field)
+        pltpu.make_async_remote_copy(
+            field.at[t, a], field_in.at[t, c, a], field_send.at[t, 1],
+            field_recv.at[t, c], partner, device_id_type=MESH,
+        ).start()
+        field_in[t, c, a] = field[t, a]
 
         @pl.when(t == 0)
         def _():
-            loads[1].wait()
-
-        partial = jnp.zeros((8, bands), F32)
+            left_copy.wait()
+
+        def two_terms(values):
+            high = values.astype(BF16).astype(F32)
+            return jnp.concatenate([high, values - high], axis=0).astype(BF16)
+
+        arrived(field_in.at[t, c, pl.ds(0, na - 1)], field_recv.at[t, c])
+        mine = two_terms(jnp.sum(field_in[t, c].astype(F32), axis=0))
+        arrived(field_in.at[t, other], field_recv.at[t, other])
+        theirs = two_terms(jnp.sum(field_in[t, other].astype(F32), axis=0))
+        partial = jnp.zeros((8, half), F32)
+        bands_at = pl.ds(pl.multiple_of(c * half, half), half)
         for k in range(4):
-            out = lax.dot_general(potential, left_v[k], NT, preferred_element_type=F32)
-            partial = partial + jnp.where(own_k(bands, k), out, 0.0)
-        half_out[t, 0] = partial[:, :half]
-        half_out[t, 1] = partial[:, half:]
-        pair = pltpu.make_async_remote_copy(
-            half_out.at[t, other], half_in.at[t], pair_send.at[t], pair_recv.at[t],
-            partner, device_id_type=MESH,
-        )
-        pair.start()
-        arrived(half_in.at[t], pair_recv.at[t])
-        direct_z[t, z] = half_out[t, c] + half_in[t]
+            out = lax.dot_general(mine, left_v[k, bands_at, :], NT, preferred_element_type=F32)
+            out += lax.dot_general(theirs, left_o[k], NT, preferred_element_type=F32)
+            partial = partial + jnp.where(own_k(half, k), out[0:8] + out[8:16], 0.0)
+        direct[t, c, z] = partial.astype(BF16)
 
         @pl.loop(1, nz)
         def _(i):
-            tz, device = z_peer(i)
-            pltpu.make_async_remote_copy(
-                direct_z.at[t, z], direct_z.at[t, z], dz_send.at[t, tz], dz_recv.at[t, z],
-                device, device_id_type=MESH,
-            ).start()
-
-        @pl.loop(1, nz)
-        def _(i):
-            tz, _d = z_peer(i)
-            arrived(direct_z.at[t, tz], dz_recv.at[t, tz])
-
-        direct_c[t, c] = jnp.sum(direct_z[t], axis=0)
-        whole = pltpu.make_async_remote_copy(
-            direct_c.at[t, c], direct_c.at[t, c], dc_send.at[t], dc_recv.at[t],
-            partner, device_id_type=MESH,
+            tz = z_near(nz - i)
+            for n, core in enumerate((c, other)):
+                pltpu.make_async_remote_copy(
+                    direct.at[t, c, z], direct.at[t, c, z], direct_send.at[t, n],
+                    direct_recv.at[t, c], (y, x, tz, core), device_id_type=MESH,
+                ).start()
+
+        pltpu.make_async_remote_copy(
+            direct.at[t, c, z], direct.at[t, c, z], direct_send.at[t, 1],
+            direct_recv.at[t, c], partner, device_id_type=MESH,
+        ).start()
+        arrived(direct.at[t, c, pl.ds(0, nz - 1)], direct_recv.at[t, c])
+        arrived(direct.at[t, other], direct_recv.at[t, other])
+        whole = jnp.concatenate(
+            [jnp.sum(direct[t, h].astype(F32), axis=0) for h in range(2)], axis=1
         )
-        whole.start()
-        arrived(direct_c.at[t, other], dc_recv.at[t])
-        direct = jnp.concatenate([direct_c[t, 0], direct_c[t, 1]], axis=1)
 
         vector = vec[...]
-        applied = levels[...] * vector - direct - beta[:, 0:1] * old[...]
+        applied = levels[...] * vector - whole - beta[:, 0:1] * old[...]
         cross = jnp.sum(vector * applied, axis=1, keepdims=True)
         square = jnp.sum(applied * applied, axis=1, keepdims=True)
         norm = jnp.sum(vector * vector, axis=1, keepdims=True)
@@ -360,15 +370,15 @@
         def _():
             send_density(t + 1, applied - share(cross, norm) * vector)
 
-        @pl.loop(1, na)
-        def _(i):
-            ta, device = plane_peer(i)
+        def send_sums(ta, ty, tx):
             pltpu.make_async_remote_copy(
-                sums.at[t, a], sums.at[t, a], sums_send.at[t, ta], sums_recv.at[t, a],
-                device, device_id_type=MESH,
+                sums.at[t, a], sums.at[t, a], sums_send.at[t], sums_recv.at[t],
+                (ty, tx, z, c), device_id_type=MESH,
             ).start()
 
-    finish(STEPS - 1, False)
+        plane_sends(send_sums)
+
+    finish(STEPS - 1)
     group = pl.ds(pl.multiple_of((b // 4) * 128, 128), 128)
     for n, source in enumerate((vec, old)):
         packed[n] = pltpu.roll(source[:, group], lax.rem(128 - lax.rem(b, 4) * 32, 128), 1)
@@ -382,11 +392,11 @@
 
     @pl.loop(0, STEPS)
     def _(t):
-        @pl.loop(1, na)
-        def _(i):
-            ta = plane_peer(i)[0]
-            sent(field.at[t, ta], field_send.at[t, ta])
-            sent(sums.at[t, a], sums_send.at[t, ta])
+        sent(field.at[t, pl.ds(0, na - 1)], field_send.at[t, 0])
+        sent(field.at[t], field_send.at[t, 1])
+        sent(sums.at[t, pl.ds(0, na - 1)], sums_send.at[t])
+        sent(direct.at[t, c, pl.ds(0, nz - 1)], direct_send.at[t, 0])
+        sent(direct.at[t, c], direct_send.at[t, 1])
 
         @pl.loop(0, nz)
         def _(tz):
@@ -397,10 +407,6 @@
         def _(i):
             tz = z_peer(i)[0]
             sent(gath.at[t, c, z, a], gz_send.at[t, tz])
-            sent(direct_z.at[t, z], dz_send.at[t, tz])
-
-        sent(half_out.at[t, other], pair_send.at[t])
-        sent(direct_c.at[t, c], dc_send.at[t])
 
 
 def unpack(packed, last, prior, alphas, betas):
@@ -438,22 +444,22 @@
             pltpu.VMEM(pair_right.shape, BF16),
             pltpu.VMEM((2, nz, nq, width, width), BF16),
             pltpu.VMEM((na * 8, nq * na * 8), BF16),
+            pltpu.VMEM((4, bands // 2, width), BF16),
             pltpu.VMEM((nz * 2, 8, 128), F32),
             pltpu.VMEM((STEPS, 2, nz, na, 8, width), BF16),
             pltpu.VMEM((nq, na * 8, width), F32),
             pltpu.VMEM((nq, na * 8, width), F32),
-            pltpu.VMEM((STEPS, na, 8, width), F32),
-            pltpu.VMEM((STEPS, na, 8, width), F32),
-            pltpu.VMEM((STEPS, 2, 8, bands // 2), F32),
-            pltpu.VMEM((STEPS, 8, bands // 2), F32),
-            pltpu.VMEM((STEPS, nz, 8, bands // 2), F32),
-            pltpu.VMEM((STEPS, 2, 8, bands // 2), F32),
+            pltpu.VMEM((STEPS, na, 8, width), BF16),
+            pltpu.VMEM((STEPS, 2, na, 8, width), BF16),
+            pltpu.VMEM((STEPS, 2, nz, 8, bands // 2), BF16),
             pltpu.VMEM((STEPS, na, 8, 128), F32),
             pltpu.VMEM((8, bands), F32),
             pltpu.VMEM((8, bands), F32),
             pltpu.VMEM((8, bands), F32),
             pltpu.VMEM((8, 128), F32),
             pltpu.VMEM((8, bands), F32),
+            pltpu.VMEM((na * 8, 128), F32),
+            pltpu.VMEM((na * 8, 128), F32),
             dma((5,)),
             dma((2 + 2 * nz,)),
             dma((nz * 2,)),
@@ -464,16 +470,14 @@
             dma((STEPS, nz)),
             dma((STEPS, nz)),
             dma((STEPS, nz)),
-            dma((STEPS, na)),
-            dma((STEPS, na)),
+            dma((STEPS, 2)),
+            dma((STEPS, 2)),
+            dma((STEPS, 2)),
+            dma((STEPS, 2)),
             dma((STEPS,)),
             dma((STEPS,)),
-            dma((STEPS, nz)),
-            dma((STEPS, nz)),
-            dma((STEPS,)),
-            dma((STEPS,)),
-            dma((STEPS, na)),
-            dma((STEPS, na)),
+            dma(()),
+            dma(()),
         ],
         compiler_params=pltpu.CompilerParams(
             collective_id=0, has_side_effects=True, vmem_limit_bytes=60 * 1024 * 1024

time: 109 us -> 101 us (0.927)
  Pallas kernels: 109 us -> 99.8 us
    pallas_call x1, Pallas kernels: 107 us -> 98.4 us  [on_device(): pl.pallas_call(functools.partial(kernel, (ny, nx, nz)), out_shape=jax.Sha...]
where the time goes in v3:
time: 101 us; the launch traced here: 100 us
  Pallas kernels  99.8 us (99%)
    pallas_call x1, Pallas kernels, on_device(): pl.pallas_call(functools.partial(kernel, (ny, nx, nz)), out_shape=jax.Sha...  98.4 us

profile of v3, /device:TPU:1, one launch (start us, length us, event | category | flops | bytes accessed | tf_op | source)
XLA Modules:
  0.0 100.4 jit_solution(15518597849600953935)
XLA Ops:
  0.6 98.4 %shard_map.111.packed = f32[4,8,128]{2,1,0:T(8,128)} custom-call(f32[4,32]{1,0:T(4,128)} %energies.1, f32[2,4,32]{2,1,0:T(4,128)} %current.1, f32[2,4,32]{2,1,0:T(4,128)} %previous.1, f32[2]{0:T(128)} %first_beta.1, s32[64,64]{1,0:T(8,128)} %momentum_h.1, bf16[4,512,256]{2,1,0:T(8,128)(2,1)} %left.1, bf16[4,512,256]{2,1,0:T(8,128)(2,1)} %right.1, ...), custom_call_target="tpu_custom_call" | custom-call | tf_op jit(solution)/shard_map/pallas_call | solution.py:432
  99.1 1.3 %shard_map.112 = (f32[2,4,32]{2,1,0:T(4,128)}, f32[2,4,32]{2,1,0:T(4,128)}, f32[2,3]{1,0:T(2,128)}, f32[2,3]{1,0:T(2,128)}) custom-call(f32[4,8,128]{2,1,0:T(8,128)} %shard_map.111.packed), custom_call_target="tpu_custom_call" | custom-call | tf_op jit(solution)/shard_map/pallas_call | solution.py:489

commit v4 on v3

--- a/solution.py
+++ b/solution.py
@@ -9,6 +9,7 @@
 from jax.sharding import PartitionSpec as P
 
 STEPS = 3
+NEAR = 1
 KPT = ("kpt_0", "kpt_1")
 PW = ("pw_0", "pw_1")
 MESH = pl.DeviceIdType.MESH
@@ -57,17 +58,9 @@
         tx = lax.rem(x + nx - lax.rem(i, nx), nx)
         return ty * nx + tx
 
-    def z_peer(i):
-        tz = lax.rem(z + i, nz)
-        return tz, (y, x, tz, c)
-
     def z_near(i):
         far, odd = (i + 1) // 2, lax.rem(i, 2)
         return lax.rem(z + odd * far + (1 - odd) * (nz - far), nz)
-
-    def pw_peer(i):
-        t = lax.rem(b + i, nz * 2)
-        return t, (y, x, t // 2, lax.rem(t, 2))
 
     partner = (y, x, z, other)
 
@@ -105,15 +98,18 @@
     def greet(device):
         pl.semaphore_signal(barrier, inc=1, device_id=device, device_id_type=MESH)
 
-    @pl.loop(1, nz * 2)
+    @pl.loop(1, nz)
     def _(i):
-        greet(pw_peer(i)[1])
+        tz = z_near(nz - i)
+        greet((y, x, tz, c))
+        greet((y, x, tz, other))
 
     def greet_both(ta, ty, tx):
         greet((ty, tx, z, c))
         greet((ty, tx, z, other))
 
     plane_sends(greet_both)
+    greet(partner)
 
     for copy in small:
         copy.wait()
@@ -145,23 +141,22 @@
         left_send, left_recv, partner, device_id_type=MESH,
     )
 
-    def pk_copy(i):
-        t, device = pw_peer(i)
-        return pltpu.make_async_remote_copy(
-            pk.at[b], pk.at[b], pk_send.at[t], pk_recv.at[b], device, device_id_type=MESH
-        )
-
     def arrived(ref, sem):
         pltpu.make_async_copy(ref, ref, sem).wait()
 
-    @pl.loop(1, nz * 2)
+    def send_pk(n, device):
+        pltpu.make_async_remote_copy(
+            pk.at[b], pk.at[b], pk_send.at[n], pk_recv.at[0], device, device_id_type=MESH
+        ).start()
+
+    @pl.loop(1, nz)
     def _(i):
-        pk_copy(i).start()
-
-    @pl.loop(1, nz * 2)
-    def _(i):
-        t, _d = pw_peer(i)
-        arrived(pk.at[t], pk_recv.at[t])
+        tz = z_near(nz - i)
+        send_pk(0, (y, x, tz, c))
+        send_pk(0, (y, x, tz, other))
+
+    send_pk(0, partner)
+    arrived(pk.at[pl.ds(0, nz * 2 - 1)], pk_recv.at[0])
 
     lane = lax.broadcasted_iota(jnp.int32, (8, 128), 1)
     for j in range(bands // 128):
@@ -208,7 +203,7 @@
             total = total + jnp.where(own_k(width, k), out[0:8] + out[8:16], 0.0)
         gath[t, c, z, a] = total.astype(BF16)
 
-        @pl.loop(1, nz)
+        @pl.loop(1, nz - 2 * NEAR)
         def _(i):
             tz = z_near(nz - i)
             pltpu.make_async_remote_copy(
@@ -226,10 +221,14 @@
 
     def finish(t):
         arrived(sums.at[t, pl.ds(0, na - 1)], sums_recv.at[t])
+        def by_row(lines, at):
+            first = lax.broadcasted_iota(jnp.int32, (*lines.shape[:-2], 8, 1), lines.ndim - 2) < 4
+            return jnp.where(first, lines[..., at : at + 1], lines[..., at + 3 : at + 4])
+
         total = jnp.sum(sums[t], axis=0)
-        cross_mean = total[:, 0:1] / entries
-        square_mean = total[:, 1:2] / entries
-        norm_mean = total[:, 2:3] / entries
+        cross_mean = by_row(total, 0) / entries
+        square_mean = by_row(total, 1) / entries
+        norm_mean = by_row(total, 2) / entries
         alpha = cross_mean
         mean_square = square_mean - 2.0 * alpha * cross_mean + alpha * alpha * norm_mean
         scale = jnp.sqrt(jnp.maximum(mean_square, 0.0) + epsilon)
@@ -239,16 +238,15 @@
         beta[...] = jnp.broadcast_to(scale, (8, 128))
         packed[2] = jnp.where(lane == t, alpha, packed[2])
         packed[3] = jnp.where(lane == t, scale, packed[3])
-        every = sums[t].reshape(nr, 128)
-        rest = jnp.broadcast_to(alpha[None], (na, 8, 128)).reshape(nr, 128)
-        rest_v[...] = rest - share(every[:, 0:1], every[:, 2:3])
+        every = sums[t]
+        shares = share(by_row(every, 0), by_row(every, 2))
+        rest_v[...] = jnp.broadcast_to(alpha[None] - shares, (na, 8, 128)).reshape(nr, 128)
         inverse_v[...] = jnp.broadcast_to((1.0 / scale)[None], (na, 8, 128)).reshape(nr, 128)
 
     packed[2] = jnp.zeros((8, 128), F32)
     packed[3] = jnp.zeros((8, 128), F32)
     rest_v[...] = jnp.zeros_like(rest_v)
     inverse_v[...] = jnp.ones_like(inverse_v)
-    images[...] = jnp.zeros_like(images)
     loads[0].wait()
     send_density(0, vec[...])
     loads[1].wait()
@@ -256,7 +254,7 @@
 
     @pl.loop(0, STEPS)
     def _(t):
-        @pl.loop(1, nz)
+        @pl.loop(1 + 2 * NEAR, nz)
         def _(i):
             tz = z_near(i)
             arrived(gath.at[t, c, tz, a], gz_recv.at[t, tz])
@@ -268,24 +266,43 @@
                 copy.wait()
 
         def forward(tz):
-            arrived(gath.at[t, c, tz, pl.ds(0, na - 1)], gx_recv.at[t, tz])
             pltpu.make_async_remote_copy(
                 gath.at[t, c, tz], gath.at[t, c, tz], fwd_send.at[t, tz], fwd_recv.at[t, tz],
                 partner, device_id_type=MESH,
             ).start()
 
+        arrived(gath.at[t, c, z, pl.ds(0, na - 1)], gx_recv.at[t, z])
+
+        @pl.loop(1, 1 + 2 * NEAR)
+        def _(i):
+            tz = z_near(i)
+            pltpu.make_async_remote_copy(
+                gath.at[t, c, z], gath.at[t, c, z], gz_send.at[t, tz], gz_recv.at[t, z],
+                (y, x, tz, c), device_id_type=MESH,
+            ).start()
+
         forward(z)
         gain(t, c, z, True)
 
-        @pl.loop(1, nz)
+        @pl.loop(1, 1 + 2 * NEAR)
         def _(i):
             tz = z_near(i)
+            arrived(gath.at[t, c, tz], gz_recv.at[t, tz])
+            forward(tz)
+            gain(t, c, tz, False)
+
+        @pl.loop(1 + 2 * NEAR, nz)
+        def _(i):
+            tz = z_near(i)
+            arrived(gath.at[t, c, tz, pl.ds(0, na - 1)], gx_recv.at[t, tz])
             forward(tz)
             gain(t, c, tz, False)
 
         @pl.when(t > 0)
         def _():
             finish(t - 1)
+            for q in range(nq):
+                gained[q] = gained[q] - rest_v[:, 0:1] * images[q]
 
         @pl.loop(0, nz)
         def _(i):
@@ -293,16 +310,14 @@
             arrived(gath.at[t, other, tz], fwd_recv.at[t, tz])
             gain(t, other, tz, False)
 
-        rest, inverse = rest_v[:, 0:1], inverse_v[:, 0:1]
-        for q in range(nq):
-            images[q] = (gained[q] - rest * images[q]) * inverse
-
-        values = images[...].reshape(nq * nr, width)
+
+        values = gained[...].reshape(nq * nr, width)
         high = values.astype(BF16)
         low = (values - high.astype(F32)).astype(BF16)
         chosen = jnp.dot(selector[...], high, preferred_element_type=F32)
         chosen = chosen + jnp.dot(selector[...], low, preferred_element_type=F32)
-        field[t] = chosen.reshape(na, 8, width).astype(BF16)
+        inverse = inverse_v[:, 0:1]
+        field[t] = (chosen * inverse).reshape(na, 8, width).astype(BF16)
 
         def send_field(ta, ty, tx):
             for n, core in enumerate((c, other)):
@@ -317,6 +332,8 @@
             field_recv.at[t, c], partner, device_id_type=MESH,
         ).start()
         field_in[t, c, a] = field[t, a]
+        for q in range(nq):
+            images[q] = gained[q] * inverse
 
         @pl.when(t == 0)
         def _():
@@ -363,7 +380,11 @@
         square = jnp.sum(applied * applied, axis=1, keepdims=True)
         norm = jnp.sum(vector * vector, axis=1, keepdims=True)
         cross, square, norm = row_total(cross), row_total(square), row_total(norm)
-        sums[t, a] = jnp.where(lane == 0, cross, jnp.where(lane == 1, square, norm))
+        line = jnp.zeros((1, 128), F32)
+        for n, value in enumerate((cross, square, norm)):
+            line = jnp.where(lane[0:1] == n, value[0:1], line)
+            line = jnp.where(lane[0:1] == n + 3, value[4:5], line)
+        sums[t, a] = line
         applied_v[...] = applied
 
         @pl.when(t < STEPS - 1)
@@ -386,9 +407,7 @@
     def sent(ref, sem):
         pltpu.make_async_copy(ref, ref, sem).wait()
 
-    @pl.loop(1, nz * 2)
-    def _(i):
-        sent(pk.at[b], pk_send.at[pw_peer(i)[0]])
+    sent(pk.at[pl.ds(0, nz * 2 - 1)], pk_send.at[0])
 
     @pl.loop(0, STEPS)
     def _(t):
@@ -398,14 +417,20 @@
         sent(direct.at[t, c, pl.ds(0, nz - 1)], direct_send.at[t, 0])
         sent(direct.at[t, c], direct_send.at[t, 1])
 
+        sent(gath.at[t, c, z, pl.ds(0, na - 1)], gx_send.at[t, z])
+
         @pl.loop(0, nz)
         def _(tz):
+            sent(gath.at[t, c, tz], fwd_send.at[t, tz])
+
+        @pl.loop(1, 1 + 2 * NEAR)
+        def _(i):
+            sent(gath.at[t, c, z], gz_send.at[t, z_near(i)])
+
+        @pl.loop(1 + 2 * NEAR, nz)
+        def _(i):
+            tz = z_near(i)
             sent(gath.at[t, c, tz, pl.ds(0, na - 1)], gx_send.at[t, tz])
-            sent(gath.at[t, c, tz], fwd_send.at[t, tz])
-
-        @pl.loop(1, nz)
-        def _(i):
-            tz = z_peer(i)[0]
             sent(gath.at[t, c, z, a], gz_send.at[t, tz])
 
 
@@ -452,7 +477,7 @@
             pltpu.VMEM((STEPS, na, 8, width), BF16),
             pltpu.VMEM((STEPS, 2, na, 8, width), BF16),
             pltpu.VMEM((STEPS, 2, nz, 8, bands // 2), BF16),
-            pltpu.VMEM((STEPS, na, 8, 128), F32),
+            pltpu.VMEM((STEPS, na, 1, 128), F32),
             pltpu.VMEM((8, bands), F32),
             pltpu.VMEM((8, bands), F32),
             pltpu.VMEM((8, bands), F32),
@@ -462,8 +487,8 @@
             pltpu.VMEM((na * 8, 128), F32),
             dma((5,)),
             dma((2 + 2 * nz,)),
-            dma((nz * 2,)),
-            dma((nz * 2,)),
+            dma((1,)),
+            dma((1,)),
             dma((STEPS, nz)),
             dma((STEPS, nz)),
             dma((STEPS, nz)),

time: 101 us -> 97.6 us (0.966)
  Pallas kernels: 99.8 us -> 96.8 us
    pallas_call x1, Pallas kernels: 98.4 us -> 95.4 us  [on_device(): pl.pallas_call(functools.partial(kernel, (ny, nx, nz)), out_shape=jax.Sha...]
where the time goes in v4:
time: 97.6 us; the launch traced here: 97.4 us
  Pallas kernels  96.8 us (99%)
    pallas_call x1, Pallas kernels, on_device(): pl.pallas_call(functools.partial(kernel, (ny, nx, nz)), out_shape=jax.Sha...  95.4 us

profile of v4, /device:TPU:1, one launch (start us, length us, event | category | flops | bytes accessed | tf_op | source)
XLA Modules:
  0.0 97.4 jit_solution(14358732754357810832)
XLA Ops:
  0.6 95.4 %shard_map.111.packed = f32[4,8,128]{2,1,0:T(8,128)} custom-call(f32[4,32]{1,0:T(4,128)} %energies.1, f32[2,4,32]{2,1,0:T(4,128)} %current.1, f32[2,4,32]{2,1,0:T(4,128)} %previous.1, f32[2]{0:T(128)} %first_beta.1, s32[64,64]{1,0:T(8,128)} %momentum_h.1, bf16[4,512,256]{2,1,0:T(8,128)(2,1)} %left.1, bf16[4,512,256]{2,1,0:T(8,128)(2,1)} %right.1, ...), custom_call_target="tpu_custom_call" | custom-call | tf_op jit(solution)/shard_map/pallas_call | solution.py:457
  96.1 1.3 %shard_map.112 = (f32[2,4,32]{2,1,0:T(4,128)}, f32[2,4,32]{2,1,0:T(4,128)}, f32[2,3]{1,0:T(2,128)}, f32[2,3]{1,0:T(2,128)}) custom-call(f32[4,8,128]{2,1,0:T(8,128)} %shard_map.111.packed), custom_call_target="tpu_custom_call" | custom-call | tf_op jit(solution)/shard_map/pallas_call | solution.py:514

commit v5 on v4

--- a/solution.py
+++ b/solution.py
@@ -25,7 +25,7 @@
     packed,
     energies_v, current_v, previous_v, first_beta_s, momentum,
     left_v, right_v, screened_v, selector,
-    left_o, pk, gath, gained, images, field, field_in, direct, sums,
+    left_o, rows, pk, gath, gained, images, field, field_in, direct, sums,
     vec, old, levels, beta, applied_v, rest_v, inverse_v,
     small_sem, load_sem, pk_send, pk_recv, gz_send, gz_recv, gx_send, gx_recv, fwd_send, fwd_recv,
     field_send, field_recv, direct_send, direct_recv, sums_send, sums_recv, left_send, left_recv,
@@ -61,6 +61,10 @@
     def z_near(i):
         far, odd = (i + 1) // 2, lax.rem(i, 2)
         return lax.rem(z + odd * far + (1 - odd) * (nz - far), nz)
+
+    def z_fixed(i):
+        far = (i + 1) // 2
+        return lax.rem(z + (far if i % 2 else nz - far), nz)
 
     partner = (y, x, z, other)
 
@@ -213,11 +217,17 @@
 
         to_plane(t, z)
 
-    def gain(t, h, tz, first):
-        block = gath[t, h, tz].astype(F32).reshape(nr, width).astype(BF16)
+    def gain(t, blocks, first=False):
+        for n, (h, tz) in enumerate(blocks):
+            rows[n] = gath[t, h, tz].astype(F32).reshape(nr, width).astype(BF16)
         for q in range(nq):
-            out = lax.dot_general(block, screened_v[h, tz, q], NT, preferred_element_type=F32)
-            gained[q] = out if first else gained[q] + out
+            total = None if first else gained[q]
+            for n, (h, tz) in enumerate(blocks):
+                out = lax.dot_general(
+                    rows[n], screened_v[h, tz, q], NT, preferred_element_type=F32
+                )
+                total = out if total is None else total + out
+            gained[q] = total
 
     def finish(t):
         arrived(sums.at[t, pl.ds(0, na - 1)], sums_recv.at[t])
@@ -282,21 +292,13 @@
             ).start()
 
         forward(z)
-        gain(t, c, z, True)
-
-        @pl.loop(1, 1 + 2 * NEAR)
-        def _(i):
-            tz = z_near(i)
-            arrived(gath.at[t, c, tz], gz_recv.at[t, tz])
-            forward(tz)
-            gain(t, c, tz, False)
-
-        @pl.loop(1 + 2 * NEAR, nz)
-        def _(i):
-            tz = z_near(i)
-            arrived(gath.at[t, c, tz, pl.ds(0, na - 1)], gx_recv.at[t, tz])
-            forward(tz)
-            gain(t, c, tz, False)
+        gain(t, [(c, z)], first=True)
+        batches = [
+            [z_fixed(i) for i in range(1, min(5, nz))],
+            [z_fixed(i) for i in range(5, nz)],
+        ]
+        arrived(gath.at[t, other, z], fwd_recv.at[t, z])
+        gain(t, [(other, z)])
 
         @pl.when(t > 0)
         def _():
@@ -304,12 +306,22 @@
             for q in range(nq):
                 gained[q] = gained[q] - rest_v[:, 0:1] * images[q]
 
-        @pl.loop(0, nz)
-        def _(i):
-            tz = z_near(i)
-            arrived(gath.at[t, other, tz], fwd_recv.at[t, tz])
-            gain(t, other, tz, False)
-
+        at = 1
+        for batch in batches:
+            for tz in batch:
+                if at <= 2 * NEAR:
+                    arrived(gath.at[t, c, tz], gz_recv.at[t, tz])
+                else:
+                    arrived(gath.at[t, c, tz, pl.ds(0, na - 1)], gx_recv.at[t, tz])
+                forward(tz)
+                at += 1
+            if batch:
+                gain(t, [(c, tz) for tz in batch])
+        for batch in batches:
+            for tz in batch:
+                arrived(gath.at[t, other, tz], fwd_recv.at[t, tz])
+            if batch:
+                gain(t, [(other, tz) for tz in batch])
 
         values = gained[...].reshape(nq * nr, width)
         high = values.astype(BF16)
@@ -470,6 +482,7 @@
             pltpu.VMEM((2, nz, nq, width, width), BF16),
             pltpu.VMEM((na * 8, nq * na * 8), BF16),
             pltpu.VMEM((4, bands // 2, width), BF16),
+            pltpu.VMEM((4, na * 8, width), BF16),
             pltpu.VMEM((nz * 2, 8, 128), F32),
             pltpu.VMEM((STEPS, 2, nz, na, 8, width), BF16),
             pltpu.VMEM((nq, na * 8, width), F32),

time: 97.6 us -> 92.8 us (0.951)
  Pallas kernels: 96.8 us -> 92 us
    pallas_call x1, Pallas kernels: 95.4 us -> 90.6 us  [on_device(): pl.pallas_call(functools.partial(kernel, (ny, nx, nz)), out_shape=jax.Sha...]
where the time goes in v5:
time: 92.8 us; the launch traced here: 92.6 us
  Pallas kernels  92 us (99%)
    pallas_call x1, Pallas kernels, on_device(): pl.pallas_call(functools.partial(kernel, (ny, nx, nz)), out_shape=jax.Sha...  90.6 us

profile of v5, /device:TPU:1, one launch (start us, length us, event | category | flops | bytes accessed | tf_op | source)
XLA Modules:
  0.0 92.6 jit_solution(16404248924273255920)
XLA Ops:
  0.6 90.6 %shard_map.111.packed = f32[4,8,128]{2,1,0:T(8,128)} custom-call(f32[4,32]{1,0:T(4,128)} %energies.1, f32[2,4,32]{2,1,0:T(4,128)} %current.1, f32[2,4,32]{2,1,0:T(4,128)} %previous.1, f32[2]{0:T(128)} %first_beta.1, s32[64,64]{1,0:T(8,128)} %momentum_h.1, bf16[4,512,256]{2,1,0:T(8,128)(2,1)} %left.1, bf16[4,512,256]{2,1,0:T(8,128)(2,1)} %right.1, ...), custom_call_target="tpu_custom_call" | custom-call | tf_op jit(solution)/shard_map/pallas_call | solution.py:469
  91.3 1.3 %shard_map.112 = (f32[2,4,32]{2,1,0:T(4,128)}, f32[2,4,32]{2,1,0:T(4,128)}, f32[2,3]{1,0:T(2,128)}, f32[2,3]{1,0:T(2,128)}) custom-call(f32[4,8,128]{2,1,0:T(8,128)} %shard_map.111.packed), custom_call_target="tpu_custom_call" | custom-call | tf_op jit(solution)/shard_map/pallas_call | solution.py:527

commit v6 on v5

--- a/solution.py
+++ b/solution.py
@@ -207,9 +207,8 @@
             total = total + jnp.where(own_k(width, k), out[0:8] + out[8:16], 0.0)
         gath[t, c, z, a] = total.astype(BF16)
 
-        @pl.loop(1, nz - 2 * NEAR)
-        def _(i):
-            tz = z_near(nz - i)
+        for i in range(nz - 1, 2 * NEAR, -1):
+            tz = z_fixed(i)
             pltpu.make_async_remote_copy(
                 gath.at[t, c, z, a], gath.at[t, c, z, a], gz_send.at[t, tz], gz_recv.at[t, z],
                 (y, x, tz, c), device_id_type=MESH,
@@ -264,9 +263,7 @@
 
     @pl.loop(0, STEPS)
     def _(t):
-        @pl.loop(1 + 2 * NEAR, nz)
-        def _(i):
-            tz = z_near(i)
+        for tz in [z_fixed(i) for i in range(1 + 2 * NEAR, nz)]:
             arrived(gath.at[t, c, tz, a], gz_recv.at[t, tz])
             to_plane(t, tz)
 
@@ -357,19 +354,19 @@
 
         arrived(field_in.at[t, c, pl.ds(0, na - 1)], field_recv.at[t, c])
         mine = two_terms(jnp.sum(field_in[t, c].astype(F32), axis=0))
-        arrived(field_in.at[t, other], field_recv.at[t, other])
-        theirs = two_terms(jnp.sum(field_in[t, other].astype(F32), axis=0))
         partial = jnp.zeros((8, half), F32)
         bands_at = pl.ds(pl.multiple_of(c * half, half), half)
         for k in range(4):
             out = lax.dot_general(mine, left_v[k, bands_at, :], NT, preferred_element_type=F32)
-            out += lax.dot_general(theirs, left_o[k], NT, preferred_element_type=F32)
+            partial = partial + jnp.where(own_k(half, k), out[0:8] + out[8:16], 0.0)
+        arrived(field_in.at[t, other], field_recv.at[t, other])
+        theirs = two_terms(jnp.sum(field_in[t, other].astype(F32), axis=0))
+        for k in range(4):
+            out = lax.dot_general(theirs, left_o[k], NT, preferred_element_type=F32)
             partial = partial + jnp.where(own_k(half, k), out[0:8] + out[8:16], 0.0)
         direct[t, c, z] = partial.astype(BF16)
 
-        @pl.loop(1, nz)
-        def _(i):
-            tz = z_near(nz - i)
+        for tz in [z_fixed(i) for i in range(nz - 1, 0, -1)]:
             for n, core in enumerate((c, other)):
                 pltpu.make_async_remote_copy(
                     direct.at[t, c, z], direct.at[t, c, z], direct_send.at[t, n],
@@ -389,19 +386,20 @@
         vector = vec[...]
         applied = levels[...] * vector - whole - beta[:, 0:1] * old[...]
         cross = jnp.sum(vector * applied, axis=1, keepdims=True)
-        square = jnp.sum(applied * applied, axis=1, keepdims=True)
         norm = jnp.sum(vector * vector, axis=1, keepdims=True)
-        cross, square, norm = row_total(cross), row_total(square), row_total(norm)
+        cross, norm = row_total(cross), row_total(norm)
+        applied_v[...] = applied
+
+        @pl.when(t < STEPS - 1)
+        def _():
+            send_density(t + 1, applied - share(cross, norm) * vector)
+
+        square = row_total(jnp.sum(applied * applied, axis=1, keepdims=True))
         line = jnp.zeros((1, 128), F32)
         for n, value in enumerate((cross, square, norm)):
             line = jnp.where(lane[0:1] == n, value[0:1], line)
             line = jnp.where(lane[0:1] == n + 3, value[4:5], line)
         sums[t, a] = line
-        applied_v[...] = applied
-
-        @pl.when(t < STEPS - 1)
-        def _():
-            send_density(t + 1, applied - share(cross, norm) * vector)
 
         def send_sums(ta, ty, tx):
             pltpu.make_async_remote_copy(

time: 92.8 us -> 93 us (level)
  no operation moved by 1% of the time
where the time goes in v6:
time: 93 us; the launch traced here: 92.8 us
  Pallas kernels  92.2 us (99%)
    pallas_call x1, Pallas kernels, on_device(): pl.pallas_call(functools.partial(kernel, (ny, nx, nz)), out_shape=jax.Sha...  90.9 us

profile of v6, /device:TPU:1, one launch (start us, length us, event | category | flops | bytes accessed | tf_op | source)
XLA Modules:
  0.0 92.8 jit_solution(14630372891962802168)
XLA Ops:
  0.6 90.9 %shard_map.111.packed = f32[4,8,128]{2,1,0:T(8,128)} custom-call(f32[4,32]{1,0:T(4,128)} %energies.1, f32[2,4,32]{2,1,0:T(4,128)} %current.1, f32[2,4,32]{2,1,0:T(4,128)} %previous.1, f32[2]{0:T(128)} %first_beta.1, s32[64,64]{1,0:T(8,128)} %momentum_h.1, bf16[4,512,256]{2,1,0:T(8,128)(2,1)} %left.1, bf16[4,512,256]{2,1,0:T(8,128)(2,1)} %right.1, ...), custom_call_target="tpu_custom_call" | custom-call | tf_op jit(solution)/shard_map/pallas_call | solution.py:467
  91.5 1.3 %shard_map.112 = (f32[2,4,32]{2,1,0:T(4,128)}, f32[2,4,32]{2,1,0:T(4,128)}, f32[2,3]{1,0:T(2,128)}, f32[2,3]{1,0:T(2,128)}) custom-call(f32[4,8,128]{2,1,0:T(8,128)} %shard_map.111.packed), custom_call_target="tpu_custom_call" | custom-call | tf_op jit(solution)/shard_map/pallas_call | solution.py:525
